TPU v7x, 8 devices: a whole 2x2x1 slice. The times are simulated.
8 devices in a mesh: dep: 2 (over z, y), col: 2 (over x), row: 2 (over core).
Axes of the slice: x: 2, y: 2, z: 1, core: 2. Of those that a mesh axis runs over, the one named last changes fastest.
Arguments:
- tokens: bfloat16 [8192, 1536], P(('dep', 'row'), 'col')
- w_up1: bfloat16 [1536, 8960], P('row', 'col')
- w_down1: bfloat16 [8960, 1536], P('row', 'col')
- w_up2: bfloat16 [1536, 8960], P('row', 'col')
- w_down2: bfloat16 [8960, 1536], P('row', 'col')
- grad_out: bfloat16 [8192, 1536], P(('dep', 'row'), 'col')
Outputs:
- output 1: bfloat16 [8192, 1536], P(('dep', 'row'), 'col')
- output 2: bfloat16 [8192, 1536], P(('dep', 'row'), 'col')
- output 3: float32 [1536, 8960], P('row', 'col')
- output 4: float32 [8960, 1536], P('row', 'col')
- output 5: float32 [1536, 8960], P('row', 'col')
- output 6: float32 [8960, 1536], P('row', 'col')
All inputs are finite; a program needn't handle non-finite values.
Results may differ from a plain program's by a relative error of at most 0.00525651.
Values are sent between devices in bfloat16 or wider.
A program may use at most 1 GiB of HBM per device.

v0:
```python
import jax
import jax.numpy as jnp
from jax import lax
from jax.sharding import PartitionSpec as P


def gelu_tanh(pre_act):
    return jax.nn.gelu(pre_act, approximate=True)


def gelu_grad(pre_act, grad_hidden):
    return jax.vjp(gelu_tanh, pre_act)[1](grad_hidden)[0]


def dot_last(left_op, right_op):
    return lax.dot_general(left_op, right_op, (((1,), (1,)), ((), ())), preferred_element_type=jnp.float32)


def dot_first(left_op, right_op):
    return lax.dot_general(left_op, right_op, (((0,), (0,)), ((), ())), preferred_element_type=jnp.float32)


def block_forward(block_in, w_up, w_down):
    acts_full = lax.all_gather(block_in, "col", axis=1, tiled=True)
    up_cols = lax.all_gather(w_up, "row", axis=0, tiled=True)
    pre_act = jnp.dot(acts_full, up_cols, preferred_element_type=jnp.float32)
    hidden = gelu_tanh(pre_act).astype(jnp.bfloat16)
    hidden_full = lax.all_gather(hidden, "col", axis=1, tiled=True)
    down_cols = lax.all_gather(w_down, "row", axis=0, tiled=True)
    mlp_out = jnp.dot(hidden_full, down_cols, preferred_element_type=jnp.float32)
    result = (block_in.astype(jnp.float32) + mlp_out).astype(jnp.bfloat16)
    return result, (acts_full, up_cols, pre_act, hidden_full, down_cols)


def block_backward(saved_acts, grad_res):
    acts_full, up_cols, pre_act, hidden_full, down_cols = saved_acts
    hidden_part = dot_last(grad_res, down_cols)
    grad_hidden = lax.psum_scatter(hidden_part, "col", scatter_dimension=1, tiled=True)
    grad_pre = gelu_grad(pre_act, grad_hidden).astype(jnp.bfloat16)
    input_part = dot_last(grad_pre, up_cols)
    input_sum = lax.psum_scatter(input_part, "col", scatter_dimension=1, tiled=True)
    grad_in = (grad_res.astype(jnp.float32) + input_sum).astype(jnp.bfloat16)
    down_part = dot_first(hidden_full, grad_res)
    grad_down = lax.psum(lax.psum_scatter(down_part, "row", scatter_dimension=0, tiled=True), "dep")
    up_part = dot_first(acts_full, grad_pre)
    grad_up = lax.psum(lax.psum_scatter(up_part, "row", scatter_dimension=0, tiled=True), "dep")
    return grad_in, grad_up, grad_down


def solution(mesh):
    act_spec = P(("dep", "row"), "col")
    weight_spec = P("row", "col")

    def local_step(tokens, w_up1, w_down1, w_up2, w_down2, grad_out):
        mid_acts, saved_first = block_forward(tokens, w_up1, w_down1)
        y_out, saved_second = block_forward(mid_acts, w_up2, w_down2)
        grad_mid, grad_up2, grad_down2 = block_backward(saved_second, grad_out)
        grad_x, grad_up1, grad_down1 = block_backward(saved_first, grad_mid)
        return y_out, grad_x, grad_up1, grad_down1, grad_up2, grad_down2

    return jax.shard_map(local_step, mesh=mesh, in_specs=(act_spec, weight_spec, weight_spec, weight_spec, weight_spec, act_spec), out_specs=(act_spec, act_spec, weight_spec, weight_spec, weight_spec, weight_spec), check_vma=False)
```

profile of v0, /device:TPU:0, one launch (start us, length us, event | category | flops | bytes accessed | tf_op | source)
XLA Modules:
  0.0 4523.3 jit_solution(2791025587953333620)
XLA Ops:
  9.4 80.5 %all-gather.9.cloned.1.call-done = bf16[2048,1536]{1,0:T(8,128)(2,1)} async-done(((bf16[2048,768]{1,0:T(8,128)(2,1)}), bf16[2048,1536]{1,0:T(8,128)(2,1)}) %all-gather.9.cloned.1.call-update) | async-done | bytes 6291472 | tf_op jit(solution)/shard_map/all_gather | solution.py:24
  89.9 24.8 all-gather.11.cloned.1.call-done
  114.7 44.5 multiply_convert_fusion.1
  160.4 422.7 %all-gather.13.cloned.1.call-done = bf16[2048,8960]{1,0:T(8,128)(2,1)} async-done(((bf16[2048,4480]{1,0:T(8,128)(2,1)}), bf16[2048,8960]{1,0:T(8,128)(2,1)}) %all-gather.13.cloned.1.call-update) | async-done | bytes 36700176 | tf_op jit(solution)/shard_map/all_gather | solution.py:28
  583.1 40.1 add_convert_fusion.3
  623.8 42.8 fusion.14
  666.9 47.5 %all-gather.17.cloned.1.call-done = bf16[2048,1536]{1,0:T(8,128)(2,1)} async-done(((bf16[2048,768]{1,0:T(8,128)(2,1)}), bf16[2048,1536]{1,0:T(8,128)(2,1)}) %all-gather.17.cloned.1.call-update) | async-done | bytes 6291472 | tf_op jit(solution)/shard_map/all_gather | solution.py:24
  714.4 795.5 %reduce-scatter.9.cloned.1.call-done = f32[2048,4480]{1,0:T(8,128)} async-done(((f32[2048,8960]{1,0:T(8,128)}), f32[2048,4480]{1,0:T(8,128)}) %reduce-scatter.9.cloned.1.call-update) | async-done | bytes 36700176 | tf_op jit(solution)/shard_map/reduce_scatter | solution.py:38
  1509.9 64.9 %fusion.13 = (bf16[2048,4480]{1,0:T(8,128)(2,1)}, bf16[2048,4480]{1,0:T(8,128)(2,1)}) fusion(f32[2048,4480]{1,0:T(8,128)} %reduce-scatter.9.cloned.1.call-done, bf16[2048,1536]{1,0:T(8,128)(2,1)} %all-gather.17.cloned.1.call-done, bf16[1536,4480]{1,0:T(8,128)(2,1)} %all-gather.19.cloned.1.call-done), kind=kOutput, calls=%fused_computation.17 | convolution fusion | flops 28387573760 | bytes 93454336 | tf_op jit(solution)/shard_map/dot_general | solution.py:26
  1574.8 38.2 fusion.15
  1613.6 141.3 %reduce-scatter.11.cloned.1.call-done = f32[2048,768]{1,0:T(8,128)} async-done(((f32[2048,1536]{1,0:T(8,128)}), f32[2048,768]{1,0:T(8,128)}) %reduce-scatter.11.cloned.1.call-update) | async-done | bytes 6291472 | tf_op jit(solution)/shard_map/reduce_scatter | solution.py:41
  1759.3 48.7 %fusion.16 = f32[2048,8960]{1,0:T(8,128)} fusion(bf16[2048,768]{1,0:T(8,128)(2,1)S(1)} %add_convert_fusion.1, bf16[8960,768]{1,0:T(8,128)(2,1)} %all-gather.15.cloned.1.call-done), kind=kOutput, calls=%fused_computation.27 | convolution fusion | flops 28185722880 | bytes 90308608 | tf_op jit(solution)/shard_map/dot_general | solution.py:16
  1808.0 37.1 fusion.19
  1845.2 35.3 fusion.18
  1880.6 298.3 %all-gather.21.cloned.1.call-done = bf16[2048,8960]{1,0:T(8,128)(2,1)} async-done(((bf16[2048,4480]{1,0:T(8,128)(2,1)}), bf16[2048,8960]{1,0:T(8,128)(2,1)}) %all-gather.21.cloned.1.call-update) | async-done | bytes 36700176 | tf_op jit(solution)/shard_map/all_gather | solution.py:28
  2178.9 35.5 fusion.20
  2214.6 759.9 %reduce-scatter.13.cloned.1.call-done = f32[2048,4480]{1,0:T(8,128)} async-done(((f32[2048,8960]{1,0:T(8,128)}), f32[2048,4480]{1,0:T(8,128)}) %reduce-scatter.13.cloned.1.call-update) | async-done | bytes 36700176 | tf_op jit(solution)/shard_map/reduce_scatter | solution.py:38
  2974.4 43.1 fusion.6
  3017.6 37.0 convolution_bitcast_fusion
  3054.7 38.7 fusion.17
  3094.6 32.7 reduce-scatter.17.cloned.1.call-done
  3127.4 38.6 add_convert_fusion.2
  3166.0 107.2 %reduce-scatter.15.cloned.1.call-done = f32[2048,768]{1,0:T(8,128)} async-done(((f32[2048,1536]{1,0:T(8,128)}), f32[2048,768]{1,0:T(8,128)}) %reduce-scatter.15.cloned.1.call-update) | async-done | bytes 6291472 | tf_op jit(solution)/shard_map/reduce_scatter | solution.py:41
  3278.3 1190.2 %all-reduce.3.cloned.1.call-done = (f32[768,4480]{0,1:T(8,128)}, f32[4480,768]{1,0:T(8,128)}, f32[768,4480]{1,0:T(8,128)}, f32[4480,768]{1,0:T(8,128)}) async-done(((f32[768,4480]{0,1:T(8,128)}, f32[4480,768]{1,0:T(8,128)}, f32[768,4480]{1,0:T(8,128)}, f32[4480,768]{1,0:T(8,128)}), (f32[768,4480]{0,1:T(8,128)}, f32[4480,768]{1,0:T(8,128)}, f32[768,4480]{1,0:T(8,128)}, ...) | async-done | bytes 55050256 | tf_op jit(solution)/shard_map/psum | solution.py:46
  (54 shorter events, 63.7 us)
Async XLA Ops:
  7.2 82.7 %all-gather.9.cloned.1.call-start = ((), (), s32[]{:S(2)}) async-start(), calls=%async_computation.8 | async-start | bytes 9437184 | tf_op jit(solution)/shard_map/all_gather | solution.py:24
  7.9 106.8 %all-gather.11.cloned.1.call-start = ((), (), s32[]{:S(2)}) async-start(), calls=%async_computation.9 | async-start | bytes 20643840 | tf_op jit(solution)/shard_map/all_gather | solution.py:25
  8.6 151.8 %all-gather.15.cloned.1.call-start = ((), (), s32[]{:S(2)}) async-start(), calls=%async_computation.11 | async-start | bytes 20643840 | tf_op jit(solution)/shard_map/all_gather | solution.py:29
  9.4 573.8 %all-gather.13.cloned.1.call-start = ((), (), s32[]{:S(2)}) async-start(), calls=%async_computation.10 | async-start | bytes 55050240 | tf_op jit(solution)/shard_map/all_gather | solution.py:28
  159.2 424.0 %copy-start.2 = (bf16[2048,768]{1,0:T(8,128)(2,1)S(1)}, bf16[2048,768]{1,0:T(8,128)(2,1)}, u32[]{:S(2)}) copy-start(bf16[2048,768]{1,0:T(8,128)(2,1)} %param.6) | copy-start | bytes 9437188
  159.2 464.6 %all-gather.23.cloned.1.call-start = ((), (), s32[]{:S(2)}) async-start(), calls=%async_computation.15 | async-start | bytes 20643840 | tf_op jit(solution)/shard_map/all_gather | solution.py:29
  159.8 507.2 %all-gather.19.cloned.1.call-start = ((), (), s32[]{:S(2)}) async-start(), calls=%async_computation.13 | async-start | bytes 20643840 | tf_op jit(solution)/shard_map/all_gather | solution.py:25
  160.3 554.1 %all-gather.17.cloned.1.call-start = ((), (), s32[]{:S(2)}) async-start(), calls=%async_computation.12 | async-start | bytes 9437184 | tf_op jit(solution)/shard_map/all_gather | solution.py:24
  623.3 886.6 %reduce-scatter.9.cloned.1.call-start = ((), (), s32[]{:S(2)}) async-start(), calls=%async_computation.16 | async-start | bytes 110100480 | tf_op jit(solution)/shard_map/reduce_scatter | solution.py:38
  666.7 1088.2 %reduce-scatter.11.cloned.1.call-start = ((), (), s32[]{:S(2)}) async-start(), calls=%async_computation.17 | async-start | bytes 18874368 | tf_op jit(solution)/shard_map/reduce_scatter | solution.py:41
  1613.0 566.0 %all-gather.21.cloned.1.call-start = ((), (), s32[]{:S(2)}) async-start(), calls=%async_computation.14 | async-start | bytes 55050240 | tf_op jit(solution)/shard_map/all_gather | solution.py:28
  1613.5 1360.9 %reduce-scatter.13.cloned.1.call-start = ((), (), s32[]{:S(2)}) async-start(), calls=%async_computation.18 | async-start | bytes 110100480 | tf_op jit(solution)/shard_map/reduce_scatter | solution.py:38
  1759.3 85.9 %copy-start = (bf16[2048,768]{1,0:T(8,128)(2,1)}, bf16[2048,768]{1,0:T(8,128)(2,1)S(1)}, u32[]{:S(2)}) copy-start(bf16[2048,768]{1,0:T(8,128)(2,1)S(1)} %add_convert_fusion.1) | copy-start | bytes 9437188
  1808.0 1285.5 %reduce-scatter.21.cloned.1.call-start = ((), (), s32[]{:S(2)}) async-start(), calls=%async_computation.22 | async-start | bytes 41287680 | tf_op jit(solution)/shard_map/reduce_scatter | solution.py:46
  1845.1 1248.3 %reduce-scatter.19.cloned.1.call-start = ((), (), s32[]{:S(2)}) async-start(), calls=%async_computation.21 | async-start | bytes 41287680 | tf_op jit(solution)/shard_map/reduce_scatter | solution.py:44
  1880.5 298.4 %copy-start.3 = (bf16[2048,768]{1,0:T(8,128)(2,1)S(1)}, bf16[2048,768]{1,0:T(8,128)(2,1)}, u32[]{:S(2)}) copy-start(bf16[2048,768]{1,0:T(8,128)(2,1)} %param.11) | copy-start | bytes 9437188
  1880.5 1214.1 %reduce-scatter.23.cloned.1.call-start = ((), (), s32[]{:S(2)}) async-start(), calls=%async_computation.23 | async-start | bytes 41287680 | tf_op jit(solution)/shard_map/reduce_scatter | solution.py:44
  2214.5 912.8 %reduce-scatter.17.cloned.1.call-start = ((), (), s32[]{:S(2)}) async-start(), calls=%async_computation.20 | async-start | bytes 41287680 | tf_op jit(solution)/shard_map/reduce_scatter | solution.py:46
  3054.6 218.6 %reduce-scatter.15.cloned.1.call-start = ((), (), s32[]{:S(2)}) async-start(), calls=%async_computation.19 | async-start | bytes 18874368 | tf_op jit(solution)/shard_map/reduce_scatter | solution.py:41
  3093.4 1375.2 %all-reduce.3.cloned.1.call-start = ((), (), s32[]{:S(2)}) async-start(), calls=%async_computation.24 | async-start | bytes 110100480 | tf_op jit(solution)/shard_map/psum | solution.py:46
  3127.3 145.8 %copy-start.1 = (bf16[2048,768]{1,0:T(8,128)(2,1)S(1)}, bf16[2048,768]{1,0:T(8,128)(2,1)}, u32[]{:S(2)}) copy-start(bf16[2048,768]{1,0:T(8,128)(2,1)} %copy-done) | copy-start | bytes 9437188
Sparse Core Ops, SparseCore 0:
  9.5 80.3 all-gather.8
  91.4 23.2 all-gather.10
  116.2 24.3 all-gather.14
  159.3 423.7 all-gather.12
  584.5 23.2 all-gather.22
  609.1 24.3 all-gather.18
  635.6 78.7 all-gather.16
  716.7 793.1 reduce-scatter.8
  1613.1 141.7 reduce-scatter.10
  1756.3 422.6 all-gather.20
  2181.2 793.1 reduce-scatter.12
  2976.6 36.9 reduce-scatter.20
  3015.8 38.3 reduce-scatter.18
  3056.3 38.3 reduce-scatter.22
  3096.8 30.5 reduce-scatter.16
  3130.0 143.1 reduce-scatter.14
  3275.6 1192.8 all-reduce.2
where the time goes:
time: 4530 us; the launch traced here: 4520 us
  waiting for transfers between devices  3910 us (86%)
  matrix products  501 us (11%)
  other arithmetic  52.7 us (1%)
  local copies, waits for them, and re-layouts  47.8 us (1%)
    reduce_scatter x2, waiting for transfers between devices, block_backward(): lax.psum_scatter(hidden_part, 'col', scatter_dimension=1, tiled=True)  1560 us
    psum x1, waiting for transfers between devices, block_backward(): lax.psum(lax.psum_scatter(up_part, 'row', scatter_dimension=0, tiled=True...  1190 us
    all_gather x2, waiting for transfers between devices, block_forward(): hidden_full = lax.all_gather(hidden, 'col', axis=1, tiled=True)  721 us
    reduce_scatter x2, waiting for transfers between devices, block_backward(): lax.psum_scatter(input_part, 'col', scatter_dimension=1, tiled=True)  248 us
    dot_general x4, matrix products, dot_last(): lax.dot_general(left_op, right_op, (((1,), (1,)), ((), ())), preferred_el...  168 us
    dot_general x4, matrix products, dot_first(): lax.dot_general(left_op, right_op, (((0,), (0,)), ((), ())), preferred_el...  145 us
    all_gather x2, waiting for transfers between devices, block_forward(): acts_full = lax.all_gather(block_in, 'col', axis=1, tiled=True)  128 us
    dot_general x2, matrix products, block_forward(): pre_act = jnp.dot(acts_full, up_cols, preferred_element_type=jnp.float32)  109 us
  transfers between devices with their start and end apart: 17, of which 12 were waited for; matrix products, arithmetic and copies ran while one was open for 10% of the time, Pallas kernels for 0%

commit v1 on v0

v1 whole, which is shorter than its diff:
```python
import jax
import jax.numpy as jnp
from jax import lax
from jax.sharding import PartitionSpec as P

LANES = 128


def gelu_tanh(pre_act):
    return jax.nn.gelu(pre_act, approximate=True)


def gelu_grad(pre_act, grad_hidden):
    return jax.vjp(gelu_tanh, pre_act)[1](grad_hidden)[0]


def dot(left_op, right_op):
    return jnp.dot(left_op, right_op, preferred_element_type=jnp.float32)


def dot_last(left_op, right_op):
    return lax.dot_general(left_op, right_op, (((1,), (1,)), ((), ())), preferred_element_type=jnp.float32)


def dot_first(left_op, right_op):
    return lax.dot_general(left_op, right_op, (((0,), (0,)), ((), ())), preferred_element_type=jnp.float32)


def swap(value, axis):
    return lax.ppermute(value, axis, [(0, 1), (1, 0)])


def half_of(value, index, axis):
    size = value.shape[axis] // 2
    return lax.dynamic_slice_in_dim(value, index * size, size, axis)


def gather_cols(value):
    return lax.all_gather(value, "col", axis=1, tiled=True)


def scatter_cols(value):
    return lax.psum_scatter(value, "col", scatter_dimension=1, tiled=True)


def in_order(index, mine, other, axis):
    low = jnp.where(index == 0, mine, other)
    high = jnp.where(index == 0, other, mine)
    return jnp.concatenate([low, high], axis=axis)


def hidden_of(acts, up):
    pre = dot(acts, up)
    return pre, gelu_tanh(pre).astype(jnp.bfloat16)


def grad_pre_of(pre, grad, down):
    return gelu_grad(pre, dot_last(grad, down)).astype(jnp.bfloat16)


def add_round(base, total):
    return (base.astype(jnp.float32) + total).astype(jnp.bfloat16)


def after(value, *others):
    return lax.optimization_barrier((value, *others))[0]


def solution(mesh):
    act_spec = P(("dep", "row"), "col")
    weight_spec = P("row", "col")

    def local_step(tokens, w_up1, w_down1, w_up2, w_down2, grad_out):
        dep = lax.axis_index("dep")
        col = lax.axis_index("col")
        row = lax.axis_index("row")
        chunk = tokens.shape[0] // 2
        ffn = w_down1.shape[0]
        window = -(-ffn // (2 * LANES)) * LANES
        start = dep * (ffn - window)
        skip = 2 * window - ffn
        last = [None]

        def run(fn, *args):
            if last[0] is not None:
                args, _ = lax.optimization_barrier((args, last[0]))
            out = fn(*args)
            last[0] = jax.tree.leaves(out)[-1]
            return out

        def win(value, axis):
            return lax.dynamic_slice_in_dim(value, start, window, axis)

        def split(value):
            return value[:chunk], value[chunk:]

        def hop(value):
            moved = lax.ppermute(value, ("dep", "col", "row"), [(1, 2), (2, 1), (5, 6), (6, 5)])
            return moved

        def hop_far(value):
            return lax.ppermute(value, ("dep", "col", "row"), [(1, 5), (5, 1), (2, 6), (6, 2)])

        def own_or(shard, moved):
            return jnp.where(col == row, shard, moved)

        def own_or_halves(shard, half, far):
            return own_or(shard, in_order(dep, half, far, 0))

        def join(mine, axis):
            other = swap(mine, "dep")
            low = jnp.where(dep == 0, mine, other)
            high = jnp.where(dep == 0, other, mine)
            high = lax.slice_in_dim(high, skip, window, axis=axis)
            return jnp.concatenate([low, high], axis=axis)

        def stack_win(near0, near1, far0, far1):
            return win(near0, 1), win(near1, 1), far0, far1

        def stack(*values):
            return jnp.concatenate(values, axis=0)

        def down_term(hids, grads, index):
            return sum(dot_first(h, half_of(g, index, 1)) for h, g in zip(hids, grads))

        def up_term(acts, gpres, index):
            return sum(dot_first(half_of(a, index, 1), g) for a, g in zip(acts, gpres))

        def plus(fn, left, right, index, received):
            return fn(left, right, index) + received

        x0, x1 = split(tokens)
        g0, g1 = split(grad_out)

        up1_other = swap(w_up1, "row")
        moved1 = hop(w_down1)
        xa0 = gather_cols(x0)
        xa1 = gather_cols(x1)
        up2_other = swap(after(w_up2, up1_other), "row")
        up1 = run(lambda a, b: in_order(row, a, b, 0), w_up1, up1_other)

        pre1_0, hid1_0 = run(hidden_of, xa0, up1)
        ga0 = gather_cols(after(g0, xa1))
        xf0 = swap(xa0, "dep")
        pre1_1, hid1_1 = run(hidden_of, xa1, up1)
        xf1 = swap(xa1, "dep")
        tile1 = run(own_or, w_down1, moved1)
        tile1_other = swap(tile1, "row")
        half2 = hop(half_of(after(w_down2, moved1), dep, 0))
        down1 = run(lambda a, b: in_order(row, a, b, 1), tile1, tile1_other)
        part0 = run(dot, hid1_0, down1)
        zs0 = scatter_cols(part0)
        part1 = run(dot, hid1_1, down1)
        zs1 = scatter_cols(part1)
        gf0 = swap(ga0, "dep")
        up2 = run(lambda a, b: in_order(row, a, b, 0), w_up2, up2_other)
        up1_win = run(lambda a: win(a, 1), up1)
        half2_far = hop_far(half2)
        hid1_f0 = run(hidden_of, xf0, up1_win)
        z0 = run(add_round, x0, zs0)
        za0 = gather_cols(z0)
        hid1_f1 = run(hidden_of, xf1, up1_win)
        tile2 = run(own_or_halves, w_down2, half2, half2_far)
        tile2_other = swap(tile2, "row")
        z1 = run(add_round, x1, zs1)
        za1 = gather_cols(z1)
        ga1 = gather_cols(after(g1, z1))
        down2 = run(lambda a, b: in_order(row, a, b, 1), tile2, tile2_other)

        zf0 = swap(za0, "dep")
        pre2, hid2_0 = run(hidden_of, za0, up2)
        gpre2_0 = run(grad_pre_of, pre2, ga0, down2)
        zf1 = swap(za1, "dep")
        ds0 = scatter_cols(run(dot_last, gpre2_0, up2))
        gf1 = swap(ga1, "dep")
        pre2, hid2_1 = run(hidden_of, za1, up2)
        gpre2_1 = run(grad_pre_of, pre2, ga1, down2)
        ds1 = scatter_cols(run(dot_last, gpre2_1, up2))

        up2_win = run(lambda a: win(a, 1), up2)
        pre2_f0, hid2_f0 = run(hidden_of, zf0, up2_win)
        pre2_f1, hid2_f1 = run(hidden_of, zf1, up2_win)
        hids2 = stack_win( hid2_0, hid2_1, hid2_f0, hid2_f1)
        grads2 = (ga0, ga1, gf0, gf1)
        sent = run(down_term, hids2, grads2, 1 - row)
        got = swap(sent, "row")
        dz0 = run(add_round, g0, ds0)
        dza0 = gather_cols(dz0)
        down_b = run(lambda *a: plus(down_term, *a), hids2, grads2, row, got)
        dz1 = run(add_round, g1, ds1)
        dza1 = gather_cols(dz1)
        down_b_moved = hop(after(down_b, dza1))
        down2_win = win(down2, 0)
        gpre2_f0 = run(grad_pre_of, pre2_f0, gf0, down2_win)
        gpre2_f1 = run(grad_pre_of, pre2_f1, gf1, down2_win)
        acts2 = (za0, za1, zf0, zf1)
        gpres2 = stack_win( gpre2_0, gpre2_1, gpre2_f0, gpre2_f1)

        dzf0 = swap(dza0, "dep")
        gpre1_0 = run(grad_pre_of, pre1_0, dza0, down1)
        xs0 = scatter_cols(run(dot_last, gpre1_0, up1))
        dzf1 = swap(dza1, "dep")
        gpre1_1 = run(grad_pre_of, pre1_1, dza1, down1)
        xs1 = scatter_cols(run(dot_last, gpre1_1, up1))

        down_b = run(lambda a, b: jnp.where(col == row, a, b), down_b, down_b_moved)
        grad_down2 = join(down_b, 0)
        sent = run(up_term, acts2, gpres2, 1 - row)
        got = swap(sent, "row")
        ys0 = scatter_cols(run(dot, hid2_0, down2))
        up_b = run(lambda *a: plus(up_term, *a), acts2, gpres2, row, got)
        grad_up2 = join(up_b, 1)

        grads1 = (dza0, dza1, dzf0, dzf1)
        hids1 = stack_win( hid1_0, hid1_1, hid1_f0[1], hid1_f1[1])
        sent = run(down_term, hids1, grads1, 1 - row)
        got = swap(sent, "row")
        down1_win = win(down1, 0)
        gpre1_f0 = run(grad_pre_of, hid1_f0[0], dzf0, down1_win)
        down_a = run(lambda *a: plus(down_term, *a), hids1, grads1, row, got)
        down_a_moved = hop(down_a)
        gpre1_f1 = run(grad_pre_of, hid1_f1[0], dzf1, down1_win)
        acts1 = (xa0, xa1, xf0, xf1)
        gpres1 = stack_win( gpre1_0, gpre1_1, gpre1_f0, gpre1_f1)
        sent = run(up_term, acts1, gpres1, 1 - row)
        got = swap(sent, "row")
        ys1 = scatter_cols(run(dot, hid2_1, down2))
        up_a = run(lambda *a: plus(up_term, *a), acts1, gpres1, row, got)
        grad_up1 = join(up_a, 1)
        down_a = run(lambda a, b: jnp.where(col == row, a, b), down_a, down_a_moved)
        grad_down1 = join(down_a, 0)
        grad_x = stack(add_round(dz0, xs0), add_round(dz1, xs1))
        y_out = stack(add_round(z0, ys0), add_round(z1, ys1))
        return y_out, grad_x, grad_up1, grad_down1, grad_up2, grad_down2

    return jax.shard_map(local_step, mesh=mesh, in_specs=(act_spec, weight_spec, weight_spec, weight_spec, weight_spec, act_spec), out_specs=(act_spec, act_spec, weight_spec, weight_spec, weight_spec, weight_spec), check_vma=False)
```

time: 4530 us -> 2050 us (0.45)
  waiting for transfers between devices: 3910 us -> 793 us
  matrix products: 501 us -> 741 us
  other arithmetic: 52.7 us -> 280 us
  starting transfers between devices: 1.32 us -> 147 us
    reduce_scatter x8, waiting for transfers between devices: 1840 us -> 0.03 us  [scatter_cols(): return lax.psum_scatter(value, 'col', scatter_dimension=1, tiled=True)]
    psum x1 -> x0, waiting for transfers between devices: 1190 us -> none  [block_backward(): lax.psum(lax.psum_scatter(up_part, 'row', scatter_dimension=0, tiled=True...]
    all_gather x8, waiting for transfers between devices: 874 us -> 239 us  [gather_cols(): return lax.all_gather(value, 'col', axis=1, tiled=True)]
    ppermute x0 -> x25, waiting for transfers between devices: none -> 552 us  [the longest x20 552 us: swap(): return lax.ppermute(value, axis, [(0, 1), (1, 0)])]
    ppermute x0 -> x25, starting transfers between devices: none -> 146 us  [the longest x20 130 us: swap(): return lax.ppermute(value, axis, [(0, 1), (1, 0)])]
    dot_general x4 -> x32, matrix products: 145 us -> 247 us  [dot_first(): lax.dot_general(left_op, right_op, (((0,), (0,)), ((), ())), preferred_el...]
    select_n x0 -> x17, other arithmetic: none -> 100 us  [the longest x5 30.8 us: in_order(): low = jnp.where(index == 0, mine, other)]
    dot_general x4 -> x12, matrix products: 168 us -> 257 us  [dot_last(): lax.dot_general(left_op, right_op, (((1,), (1,)), ((), ())), preferred_el...]
  transfers between devices with their start and end apart: 17 -> 41, of which waited for: 12 -> 16; matrix products, arithmetic and copies ran while one was open for 10% -> 46% of each run, Pallas kernels for 0% -> 0%
where the time goes in v1:
time: 2050 us
  waiting for transfers between devices  793 us (39%)
  matrix products  741 us (36%)
  other arithmetic  280 us (14%)
  starting transfers between devices  147 us (7%)
  local copies, waits for them, and re-layouts  70.2 us (3%)
    ppermute x20, waiting for transfers between devices, swap(): return lax.ppermute(value, axis, [(0, 1), (1, 0)])  552 us
    dot_general x12, matrix products, dot_last(): lax.dot_general(left_op, right_op, (((1,), (1,)), ((), ())), preferred_el...  257 us
    dot_general x32, matrix products, dot_first(): lax.dot_general(left_op, right_op, (((0,), (0,)), ((), ())), preferred_el...  247 us
    all_gather x8, waiting for transfers between devices, gather_cols(): return lax.all_gather(value, 'col', axis=1, tiled=True)  239 us
    dot_general x12, matrix products, dot(): return jnp.dot(left_op, right_op, preferred_element_type=jnp.float32)  237 us
    ppermute x20, starting transfers between devices, swap(): return lax.ppermute(value, axis, [(0, 1), (1, 0)])  130 us
    add x4, other arithmetic, plus(): return fn(left, right, index) + received  56.9 us
    dynamic_slice x8, local copies, waits for them, and re-layouts, win(): return lax.dynamic_slice_in_dim(value, start, window, axis)  44.2 us
  transfers between devices with their start and end apart: 41, of which 16 were waited for; matrix products, arithmetic and copies ran while one was open for 46% of the time, Pallas kernels for 0%

profile of v1, /device:TPU:0, one launch (start us, length us, event | category | flops | bytes accessed | tf_op | source)
XLA Modules:
  0.0 2045.4 jit_solution(16533633417179568454)
XLA Ops:
  31.2 42.1 %all-gather.9.cloned.1.call-done = bf16[1024,1536]{1,0:T(8,128)(2,1)} async-done(((bf16[1024,768]{1,0:T(8,128)(2,1)}), bf16[1024,1536]{1,0:T(8,128)(2,1)}) %all-gather.9.cloned.1.call-update) | async-done | bytes 3145744 | tf_op jit(solution)/shard_map/all_gather | solution.py:39
  73.2 24.4 %fusion.35 = (bf16[1024,4480]{1,0:T(8,128)(2,1)}, f32[1024,4480]{1,0:T(8,128)}) fusion(bf16[1024,1536]{1,0:T(8,128)(2,1)} %all-gather.9.cloned.1.call-done, bf16[1536,4480]{1,0:T(8,128)(2,1)} %pad_maximum_fusion.2), kind=kOutput, calls=%fused_computation.47 | convolution fusion | flops 14134149120 | bytes 44433408 | tf_op jit(solution)/shard_map/dot_general | solution.py:18
  97.6 36.8 %all-gather.11.cloned.1.call-done = bf16[1024,1536]{1,0:T(8,128)(2,1)} async-done(((bf16[1024,768]{1,0:T(8,128)(2,1)}), bf16[1024,1536]{1,0:T(8,128)(2,1)}) %all-gather.11.cloned.1.call-update) | async-done | bytes 3145744 | tf_op jit(solution)/shard_map/all_gather | solution.py:39
  134.4 24.4 %fusion.43 = (bf16[1024,4480]{1,0:T(8,128)(2,1)}, f32[1024,4480]{1,0:T(8,128)}) fusion(bf16[1024,1536]{1,0:T(8,128)(2,1)} %all-gather.11.cloned.1.call-done, bf16[1536,4480]{1,0:T(8,128)(2,1)} %pad_maximum_fusion.2), kind=kOutput, calls=%fused_computation.55 | convolution fusion | flops 14134149120 | bytes 44433408 | tf_op jit(solution)/shard_map/dot_general | solution.py:18
  209.7 21.9 %fusion.229 = f32[1024,1536]{1,0:T(8,128)} fusion(bf16[1024,4480]{1,0:T(8,128)(2,1)} %get-tuple-element.179, bf16[4480,1536]{1,0:T(8,128)(2,1)} %copy-done.10), kind=kOutput, calls=%fused_computation.308 | convolution fusion | flops 14092861440 | bytes 29229056 | tf_op jit(solution)/shard_map/dot_general | solution.py:18
  262.2 117.3 %collective-permute-done.3 = bf16[1024,1536]{1,0:T(8,128)(2,1)} collective-permute-done((bf16[1024,1536]{1,0:T(8,128)(2,1)}, bf16[1024,1536]{1,0:T(8,128)(2,1)}, u32[]{:S(2)}, u32[]{:S(2)}) %collective-permute-start.3) | collective-permute-done | bytes 3145760 | tf_op jit(solution)/shard_map/ppermute | solution.py:30
  436.6 40.2 %all-gather.13.cloned.1.call-done = bf16[1024,1536]{1,0:T(8,128)(2,1)} async-done(((bf16[1024,768]{1,0:T(8,128)(2,1)}), bf16[1024,1536]{1,0:T(8,128)(2,1)}) %all-gather.13.cloned.1.call-update) | async-done | bytes 3145744 | tf_op jit(solution)/shard_map/all_gather | solution.py:39
  478.3 42.8 %all-gather.15.cloned.1.call-done = bf16[1024,1536]{1,0:T(8,128)(2,1)} async-done(((bf16[1024,768]{1,0:T(8,128)(2,1)}), bf16[1024,1536]{1,0:T(8,128)(2,1)}) %all-gather.15.cloned.1.call-update) | async-done | bytes 3145744 | tf_op jit(solution)/shard_map/all_gather | solution.py:39
  522.6 42.2 %all-gather.19.cloned.1.call-done = bf16[1024,1536]{1,0:T(8,128)(2,1)} async-done(((bf16[1024,768]{1,0:T(8,128)(2,1)}), bf16[1024,1536]{1,0:T(8,128)(2,1)}) %all-gather.19.cloned.1.call-update) | async-done | bytes 3145744 | tf_op jit(solution)/shard_map/all_gather | solution.py:39
  605.2 30.4 %fusion.6 = bf16[1024,4480]{1,0:T(8,128)(2,1)} fusion(f32[1024,4480]{1,0:T(8,128)} %get-tuple-element.203, bf16[1024,1536]{1,0:T(8,128)(2,1)S(1)} %copy-done.21, bf16[4480,1536]{1,0:T(8,128)(2,1)} %pad_maximum_fusion.1), kind=kOutput, calls=%fused_computation.18 | convolution fusion | flops 14184611840 | bytes 44433408 | tf_op jit(solution)/shard_map/dot_general | solution.py:22
  635.6 21.9 %fusion.230 = f32[1024,1536]{1,0:T(8,128)} fusion(bf16[1024,4480]{1,0:T(8,128)(2,1)} %fusion.6, bf16[1536,4480]{1,0:T(8,128)(2,1)} %pad_maximum_fusion.3), kind=kOutput, calls=%fused_computation.309 | convolution fusion | flops 14092861440 | bytes 29229056 | tf_op jit(solution)/shard_map/dot_general | solution.py:22
  657.6 24.0 %fusion.59 = (bf16[1024,4480]{1,0:T(8,128)(2,1)}, f32[1024,4480]{1,0:T(8,128)}) fusion(bf16[1024,1536]{1,0:T(8,128)(2,1)S(1)} %copy-done.18, bf16[1536,4480]{1,0:T(8,128)(2,1)} %pad_maximum_fusion.3), kind=kOutput, calls=%fused_computation.71 | convolution fusion | flops 14134149120 | bytes 44433408 | tf_op jit(solution)/shard_map/dot_general | solution.py:18
  681.6 30.3 %fusion.13 = bf16[1024,4480]{1,0:T(8,128)(2,1)} fusion(f32[1024,4480]{1,0:T(8,128)} %get-tuple-element.211, bf16[1024,1536]{1,0:T(8,128)(2,1)S(1)} %copy-done.26, bf16[4480,1536]{1,0:T(8,128)(2,1)} %pad_maximum_fusion.1), kind=kOutput, calls=%fused_computation.25 | convolution fusion | flops 14184611840 | bytes 44433408 | tf_op jit(solution)/shard_map/dot_general | solution.py:22
  711.8 21.9 %fusion.231 = f32[1024,1536]{1,0:T(8,128)} fusion(bf16[1024,4480]{1,0:T(8,128)(2,1)} %fusion.13, bf16[1536,4480]{1,0:T(8,128)(2,1)} %pad_maximum_fusion.3), kind=kOutput, calls=%fused_computation.310 | convolution fusion | flops 14092861440 | bytes 29229056 | tf_op jit(solution)/shard_map/dot_general | solution.py:22
  916.2 35.2 %all-gather.23.cloned.1.call-done = bf16[1024,1536]{1,0:T(8,128)(2,1)} async-done(((bf16[1024,768]{1,0:T(8,128)(2,1)}), bf16[1024,1536]{1,0:T(8,128)(2,1)}) %all-gather.23.cloned.1.call-update) | async-done | bytes 3145744 | tf_op jit(solution)/shard_map/all_gather | solution.py:39
  951.3 31.4 %fusion.20 = bf16[1024,4480]{1,0:T(8,128)(2,1)} fusion(f32[1024,4480]{1,0:T(8,128)} %get-tuple-element.251, bf16[1024,1536]{1,0:T(8,128)(2,1)} %all-gather.23.cloned.1.call-done, bf16[4480,1536]{1,0:T(8,128)(2,1)} %copy-done.10), kind=kOutput, calls=%fused_computation.32 | convolution fusion | flops 14184611840 | bytes 44433408 | tf_op jit(solution)/shard_map/dot_general | solution.py:22
  1004.5 30.6 %fusion.27 = bf16[1024,4480]{1,0:T(8,128)(2,1)} fusion(f32[1024,4480]{1,0:T(8,128)} %get-tuple-element.256, bf16[1024,1536]{1,0:T(8,128)(2,1)S(1)} %copy-done.23, bf16[4480,1536]{1,0:T(8,128)(2,1)} %copy-done.10), kind=kOutput, calls=%fused_computation.39 | convolution fusion | flops 14184611840 | bytes 44433408 | tf_op jit(solution)/shard_map/dot_general | solution.py:22
  1112.6 112.8 %collective-permute-start.17 = (f32[768,2304]{1,0:T(8,128)}, f32[768,2304]{1,0:T(8,128)}, u32[]{:S(2)}, u32[]{:S(2)}) collective-permute-start(f32[768,2304]{1,0:T(8,128)} %add_add_fusion.5), channel_id=1, source_target_pairs={{0,1},{1,0},{2,3},{3,2},{4,5},{5,4},{6,7},{7,6}} | collective-permute-start | bytes 21233672 | tf_op jit(solution)/shard_map/ppermute | solution.py:30
  1234.0 22.7 %fusion.236 = f32[1024,1536]{1,0:T(8,128)} fusion(bf16[1024,4480]{1,0:T(8,128)(2,1)} %get-tuple-element.270, bf16[4480,1536]{1,0:T(8,128)(2,1)} %pad_maximum_fusion.1), kind=kOutput, calls=%fused_computation.315 | convolution fusion | flops 14092861440 | bytes 29229056 | tf_op jit(solution)/shard_map/dot_general | solution.py:18
  1303.3 66.5 %collective-permute-done.16 = bf16[1024,1536]{1,0:T(8,128)(2,1)} collective-permute-done((bf16[1024,1536]{1,0:T(8,128)(2,1)}, bf16[1024,1536]{1,0:T(8,128)(2,1)}, u32[]{:S(2)}, u32[]{:S(2)}) %collective-permute-start.16) | collective-permute-done | bytes 3145760 | tf_op jit(solution)/shard_map/ppermute | solution.py:30
  1547.0 22.2 %collective-permute-done.24 = f32[2304,768]{1,0:T(8,128)} collective-permute-done((f32[2304,768]{1,0:T(8,128)}, f32[2304,768]{1,0:T(8,128)}, u32[]{:S(2)}, u32[]{:S(2)}) %collective-permute-start.24) | collective-permute-done | bytes 7077920 | tf_op jit(solution)/shard_map/ppermute | solution.py:30
  1672.6 48.3 %collective-permute-done.23 = f32[768,2304]{1,0:T(8,128)} collective-permute-done((f32[768,2304]{1,0:T(8,128)}, f32[768,2304]{1,0:T(8,128)}, u32[]{:S(2)}, u32[]{:S(2)}) %collective-permute-start.23) | collective-permute-done | bytes 7077920 | tf_op jit(solution)/shard_map/ppermute | solution.py:30
  1740.6 132.0 %collective-permute-done.20 = f32[768,2304]{1,0:T(8,128)} collective-permute-done((f32[768,2304]{1,0:T(8,128)}, f32[768,2304]{1,0:T(8,128)}, u32[]{:S(2)}, u32[]{:S(2)}) %collective-permute-start.20) | collective-permute-done | bytes 7077920 | tf_op jit(solution)/shard_map/ppermute | solution.py:30
  1887.3 136.5 %collective-permute-done.22 = f32[2304,768]{1,0:T(8,128)} collective-permute-done((f32[2304,768]{1,0:T(8,128)}, f32[2304,768]{1,0:T(8,128)}, u32[]{:S(2)}, u32[]{:S(2)}) %collective-permute-start.22) | collective-permute-done | bytes 7077920 | tf_op jit(solution)/shard_map/ppermute | solution.py:30
  (434 shorter events, 871.5 us)
Async XLA Ops:
  11.9 146.9 %collective-permute-start.1 = (bf16[4480,768]{1,0:T(8,128)(2,1)}, bf16[4480,768]{1,0:T(8,128)(2,1)}, u32[]{:S(2)}, u32[]{:S(2)}) collective-permute-start(bf16[4480,768]{1,0:T(8,128)(2,1)} %param.8), channel_id=1, source_target_pairs={{1,2},{2,1},{5,6},{6,5}} | collective-permute-start | bytes 20643848 | tf_op jit(solution)/shard_map/ppermute | solution.py:98
  15.4 379.4 %reduce-scatter.9.cloned.1.call-start = ((), (), s32[]{:S(2)}) async-start(), calls=%async_computation.10 | async-start | bytes 9437184 | tf_op jit(solution)/shard_map/reduce_scatter | solution.py:43
  209.6 220.9 %reduce-scatter.11.cloned.1.call-start = ((), (), s32[]{:S(2)}) async-start(), calls=%async_computation.12 | async-start | bytes 9437184 | tf_op jit(solution)/shard_map/reduce_scatter | solution.py:43
  231.7 203.1 %all-gather.17.cloned.1.call-start = ((), (), s32[]{:S(2)}) async-start(), calls=%async_computation.14 | async-start | bytes 4718592 | tf_op jit(solution)/shard_map/all_gather | solution.py:39
  240.3 236.6 %all-gather.13.cloned.1.call-start = ((), (), s32[]{:S(2)}) async-start(), calls=%async_computation.11 | async-start | bytes 4718592 | tf_op jit(solution)/shard_map/all_gather | solution.py:39
  240.3 158.4 %collective-permute-start.7 = (bf16[1024,1536]{1,0:T(8,128)(2,1)}, bf16[1024,1536]{1,0:T(8,128)(2,1)}, u32[]{:S(2)}, u32[]{:S(2)}) collective-permute-start(bf16[1024,1536]{1,0:T(8,128)(2,1)} %all-gather.11.cloned.1.call-done), channel_id=1, source_target_pairs={{0,4},{4,0},{1,5},{5,1},{2,6},{6,2},{3,7},{7,3}} | collective-permute-start | bytes 9437192 | tf_op jit(solution)/shard_map/ppermute | solution.py:30
  242.9 136.5 %collective-permute-start.3 = (bf16[1024,1536]{1,0:T(8,128)(2,1)}, bf16[1024,1536]{1,0:T(8,128)(2,1)}, u32[]{:S(2)}, u32[]{:S(2)}) collective-permute-start(bf16[1024,1536]{1,0:T(8,128)(2,1)} %all-gather.9.cloned.1.call-done), channel_id=1, source_target_pairs={{0,4},{4,0},{1,5},{5,1},{2,6},{6,2},{3,7},{7,3}} | collective-permute-start | bytes 9437192 | tf_op jit(solution)/shard_map/ppermute | solution.py:30
  243.0 171.5 %collective-permute-start.6 = (bf16[2240,768]{1,0:T(8,128)(2,1)}, bf16[2240,768]{1,0:T(8,128)(2,1)}, u32[]{:S(2)}, u32[]{:S(2)}) collective-permute-start(bf16[2240,768]{1,0:T(8,128)(2,1)} %collective-permute-done.5), channel_id=1, source_target_pairs={{1,5},{5,1},{2,6},{6,2}} | collective-permute-start | bytes 10321928 | tf_op jit(solution)/shard_map/ppermute | solution.py:102
  434.7 376.3 %reduce-scatter.15.cloned.1.call-start = ((), (), s32[]{:S(2)}) async-start(), calls=%async_computation.17 | async-start | bytes 9437184 | tf_op jit(solution)/shard_map/reduce_scatter | solution.py:43
  434.7 345.3 %collective-permute-start.11 = (bf16[1024,1536]{1,0:T(8,128)(2,1)}, bf16[1024,1536]{1,0:T(8,128)(2,1)}, u32[]{:S(2)}, u32[]{:S(2)}) collective-permute-start(bf16[1024,1536]{1,0:T(8,128)(2,1)} %all-gather.17.cloned.1.call-done), channel_id=1, source_target_pairs={{0,4},{4,0},{1,5},{5,1},{2,6},{6,2},{3,7},{7,3}} | collective-permute-start | bytes 9437192 | tf_op jit(solution)/shard_map/ppermute | solution.py:30
  476.9 263.2 %collective-permute-start.9 = (bf16[1024,1536]{1,0:T(8,128)(2,1)}, bf16[1024,1536]{1,0:T(8,128)(2,1)}, u32[]{:S(2)}, u32[]{:S(2)}) collective-permute-start(bf16[1024,1536]{1,0:T(8,128)(2,1)} %all-gather.13.cloned.1.call-done), channel_id=1, source_target_pairs={{0,4},{4,0},{1,5},{5,1},{2,6},{6,2},{3,7},{7,3}} | collective-permute-start | bytes 9437192 | tf_op jit(solution)/shard_map/ppermute | solution.py:30
  521.1 235.5 %collective-permute-start.10 = (bf16[1024,1536]{1,0:T(8,128)(2,1)}, bf16[1024,1536]{1,0:T(8,128)(2,1)}, u32[]{:S(2)}, u32[]{:S(2)}) collective-permute-start(bf16[1024,1536]{1,0:T(8,128)(2,1)} %all-gather.15.cloned.1.call-done), channel_id=1, source_target_pairs={{0,4},{4,0},{1,5},{5,1},{2,6},{6,2},{3,7},{7,3}} | collective-permute-start | bytes 9437192 | tf_op jit(solution)/shard_map/ppermute | solution.py:30
  564.8 215.3 %collective-permute-start.12 = (bf16[1024,1536]{1,0:T(8,128)(2,1)}, bf16[1024,1536]{1,0:T(8,128)(2,1)}, u32[]{:S(2)}, u32[]{:S(2)}) collective-permute-start(bf16[1024,1536]{1,0:T(8,128)(2,1)} %all-gather.19.cloned.1.call-done), channel_id=1, source_target_pairs={{0,4},{4,0},{1,5},{5,1},{2,6},{6,2},{3,7},{7,3}} | collective-permute-start | bytes 9437192 | tf_op jit(solution)/shard_map/ppermute | solution.py:30
  657.5 205.9 %reduce-scatter.13.cloned.1.call-start = ((), (), s32[]{:S(2)}) async-start(), calls=%async_computation.16 | async-start | bytes 9437184 | tf_op jit(solution)/shard_map/reduce_scatter | solution.py:43
  740.1 176.0 %all-gather.21.cloned.1.call-start = ((), (), s32[]{:S(2)}) async-start(), calls=%async_computation.18 | async-start | bytes 4718592 | tf_op jit(solution)/shard_map/all_gather | solution.py:39
  874.1 541.0 %reduce-scatter.23.cloned.1.call-start = ((), (), s32[]{:S(2)}) async-start(), calls=%async_computation.23 | async-start | bytes 9437184 | tf_op jit(solution)/shard_map/reduce_scatter | solution.py:43
  1060.2 358.3 %reduce-scatter.21.cloned.1.call-start = ((), (), s32[]{:S(2)}) async-start(), calls=%async_computation.22 | async-start | bytes 9437184 | tf_op jit(solution)/shard_map/reduce_scatter | solution.py:43
  1112.6 144.2 %collective-permute-start.17 = (f32[768,2304]{1,0:T(8,128)}, f32[768,2304]{1,0:T(8,128)}, u32[]{:S(2)}, u32[]{:S(2)}) collective-permute-start(f32[768,2304]{1,0:T(8,128)} %add_add_fusion.5), channel_id=1, source_target_pairs={{0,1},{1,0},{2,3},{3,2},{4,5},{5,4},{6,7},{7,6}} | collective-permute-start | bytes 21233672 | tf_op jit(solution)/shard_map/ppermute | solution.py:30
  1231.9 429.0 %reduce-scatter.17.cloned.1.call-start = ((), (), s32[]{:S(2)}) async-start(), calls=%async_computation.20 | async-start | bytes 9437184 | tf_op jit(solution)/shard_map/reduce_scatter | solution.py:43
  1413.6 155.6 %collective-permute-start.24 = (f32[2304,768]{1,0:T(8,128)}, f32[2304,768]{1,0:T(8,128)}, u32[]{:S(2)}, u32[]{:S(2)}) collective-permute-start(f32[2304,768]{1,0:T(8,128)} %broadcast_select_fusion.14), channel_id=1, source_target_pairs={{0,4},{4,0},{1,5},{5,1},{2,6},{6,2},{3,7},{7,3}} | collective-permute-start | bytes 21233672 | tf_op jit(solution)/shard_map/ppermute | solution.py:30
  1415.0 320.8 %reduce-scatter.19.cloned.1.call-start = ((), (), s32[]{:S(2)}) async-start(), calls=%async_computation.21 | async-start | bytes 9437184 | tf_op jit(solution)/shard_map/reduce_scatter | solution.py:43
  1423.1 297.8 %collective-permute-start.23 = (f32[768,2304]{1,0:T(8,128)}, f32[768,2304]{1,0:T(8,128)}, u32[]{:S(2)}, u32[]{:S(2)}) collective-permute-start(f32[768,2304]{1,0:T(8,128)} %add_add_fusion.4), channel_id=1, source_target_pairs={{0,4},{4,0},{1,5},{5,1},{2,6},{6,2},{3,7},{7,3}} | collective-permute-start | bytes 21233672 | tf_op jit(solution)/shard_map/ppermute | solution.py:30
  1654.2 218.4 %collective-permute-start.20 = (f32[768,2304]{1,0:T(8,128)}, f32[768,2304]{1,0:T(8,128)}, u32[]{:S(2)}, u32[]{:S(2)}) collective-permute-start(f32[768,2304]{1,0:T(8,128)} %add_add_fusion), channel_id=1, source_target_pairs={{0,4},{4,0},{1,5},{5,1},{2,6},{6,2},{3,7},{7,3}} | collective-permute-start | bytes 21233672 | tf_op jit(solution)/shard_map/ppermute | solution.py:30
  1672.0 351.8 %collective-permute-start.22 = (f32[2304,768]{1,0:T(8,128)}, f32[2304,768]{1,0:T(8,128)}, u32[]{:S(2)}, u32[]{:S(2)}) collective-permute-start(f32[2304,768]{1,0:T(8,128)} %broadcast_select_fusion.13), channel_id=1, source_target_pairs={{0,4},{4,0},{1,5},{5,1},{2,6},{6,2},{3,7},{7,3}} | collective-permute-start | bytes 21233672 | tf_op jit(solution)/shard_map/ppermute | solution.py:30
  (124 other events, 3019.7 us)
Sparse Core Ops, SparseCore 0:
  12.0 61.2 all-gather.8
  75.3 59.0 all-gather.10
  209.8 97.9 reduce-scatter.8
  309.9 79.9 reduce-scatter.10
  391.2 42.1 all-gather.16
  434.7 42.1 all-gather.12
  479.0 42.1 all-gather.14
  522.6 42.1 all-gather.18
  657.6 73.4 reduce-scatter.14
  740.3 73.2 reduce-scatter.12
  866.9 40.8 all-gather.20
  909.2 42.1 all-gather.22
  1060.3 108.1 reduce-scatter.22
  1232.0 74.7 reduce-scatter.20
  1415.2 74.2 reduce-scatter.16
  1601.2 108.0 reduce-scatter.18

commit v2 on v1

--- a/solution.py
+++ b/solution.py
@@ -114,17 +114,13 @@
             high = lax.slice_in_dim(high, skip, window, axis=axis)
             return jnp.concatenate([low, high], axis=axis)
 
-        def stack_win(near0, near1, far0, far1):
-            return win(near0, 1), win(near1, 1), far0, far1
-
-        def stack(*values):
-            return jnp.concatenate(values, axis=0)
-
         def down_term(hids, grads, index):
-            return sum(dot_first(h, half_of(g, index, 1)) for h, g in zip(hids, grads))
+            near, far = ([dot_first(h, half_of(g, index, 1)) for h, g in zip(*p)] for p in zip(hids, grads))
+            return (near[0] + near[1]) + (far[0] + far[1])
 
         def up_term(acts, gpres, index):
-            return sum(dot_first(half_of(a, index, 1), g) for a, g in zip(acts, gpres))
+            near, far = ([dot_first(half_of(a, index, 1), g) for a, g in zip(*p)] for p in zip(acts, gpres))
+            return (near[0] + near[1]) + (far[0] + far[1])
 
         def plus(fn, left, right, index, received):
             return fn(left, right, index) + received
@@ -154,12 +150,11 @@
         zs1 = scatter_cols(part1)
         gf0 = swap(ga0, "dep")
         up2 = run(lambda a, b: in_order(row, a, b, 0), w_up2, up2_other)
-        up1_win = run(lambda a: win(a, 1), up1)
         half2_far = hop_far(half2)
-        hid1_f0 = run(hidden_of, xf0, up1_win)
+        hid1_f0 = run(hidden_of, xf0, up1)
         z0 = run(add_round, x0, zs0)
         za0 = gather_cols(z0)
-        hid1_f1 = run(hidden_of, xf1, up1_win)
+        hid1_f1 = run(hidden_of, xf1, up1)
         tile2 = run(own_or_halves, w_down2, half2, half2_far)
         tile2_other = swap(tile2, "row")
         z1 = run(add_round, x1, zs1)
@@ -170,9 +165,10 @@
         zf0 = swap(za0, "dep")
         pre2, hid2_0 = run(hidden_of, za0, up2)
         gpre2_0 = run(grad_pre_of, pre2, ga0, down2)
-        zf1 = swap(za1, "dep")
-        ds0 = scatter_cols(run(dot_last, gpre2_0, up2))
-        gf1 = swap(ga1, "dep")
+        zf1 = swap(after(za1, gpre2_0), "dep")
+        part0 = run(dot_last, gpre2_0, up2)
+        ds0 = scatter_cols(part0)
+        gf1 = swap(after(ga1, part0), "dep")
         pre2, hid2_1 = run(hidden_of, za1, up2)
         gpre2_1 = run(grad_pre_of, pre2, ga1, down2)
         ds1 = scatter_cols(run(dot_last, gpre2_1, up2))
@@ -180,57 +176,56 @@
         up2_win = run(lambda a: win(a, 1), up2)
         pre2_f0, hid2_f0 = run(hidden_of, zf0, up2_win)
         pre2_f1, hid2_f1 = run(hidden_of, zf1, up2_win)
-        hids2 = stack_win( hid2_0, hid2_1, hid2_f0, hid2_f1)
-        grads2 = (ga0, ga1, gf0, gf1)
-        sent = run(down_term, hids2, grads2, 1 - row)
-        got = swap(sent, "row")
         dz0 = run(add_round, g0, ds0)
         dza0 = gather_cols(dz0)
-        down_b = run(lambda *a: plus(down_term, *a), hids2, grads2, row, got)
-        dz1 = run(add_round, g1, ds1)
-        dza1 = gather_cols(dz1)
-        down_b_moved = hop(after(down_b, dza1))
         down2_win = win(down2, 0)
         gpre2_f0 = run(grad_pre_of, pre2_f0, gf0, down2_win)
         gpre2_f1 = run(grad_pre_of, pre2_f1, gf1, down2_win)
-        acts2 = (za0, za1, zf0, zf1)
-        gpres2 = stack_win( gpre2_0, gpre2_1, gpre2_f0, gpre2_f1)
-
+        acts2 = (za0, za1), (zf0, zf1)
+        gpres2 = (win(gpre2_0, 1), win(gpre2_1, 1)), (gpre2_f0, gpre2_f1)
+        sent = run(up_term, acts2, gpres2, 1 - row)
+        got = swap(sent, "row")
+        dz1 = run(add_round, g1, ds1)
+        dza1 = gather_cols(dz1)
         dzf0 = swap(dza0, "dep")
+        up_b = run(lambda *a: plus(up_term, *a), acts2, gpres2, row, got)
+        dzf1 = swap(dza1, "dep")
+        hids2 = (win(hid2_0, 1), win(hid2_1, 1)), (hid2_f0, hid2_f1)
+        grads2 = (ga0, ga1), (gf0, gf1)
+        sent = run(down_term, hids2, grads2, 1 - row)
+        got = swap(sent, "row")
+        grad_up2 = join(after(up_b, sent), 1)
+        ys0 = scatter_cols(run(dot, hid2_0, down2))
+        down_b = run(lambda *a: plus(down_term, *a), hids2, grads2, row, got)
+        down_b_moved = hop(after(down_b, dza1))
+        ys1 = scatter_cols(run(dot, hid2_1, down2))
+
         gpre1_0 = run(grad_pre_of, pre1_0, dza0, down1)
         xs0 = scatter_cols(run(dot_last, gpre1_0, up1))
-        dzf1 = swap(dza1, "dep")
         gpre1_1 = run(grad_pre_of, pre1_1, dza1, down1)
+        grads1 = (dza0, dza1), (dzf0, dzf1)
+        hids1 = (hid1_0, hid1_1), (hid1_f0[1], hid1_f1[1])
+        sent = run(down_term, hids1, grads1, 1 - row)
+        got = swap(sent, "row")
         xs1 = scatter_cols(run(dot_last, gpre1_1, up1))
-
-        down_b = run(lambda a, b: jnp.where(col == row, a, b), down_b, down_b_moved)
-        grad_down2 = join(down_b, 0)
-        sent = run(up_term, acts2, gpres2, 1 - row)
-        got = swap(sent, "row")
-        ys0 = scatter_cols(run(dot, hid2_0, down2))
-        up_b = run(lambda *a: plus(up_term, *a), acts2, gpres2, row, got)
-        grad_up2 = join(up_b, 1)
-
-        grads1 = (dza0, dza1, dzf0, dzf1)
-        hids1 = stack_win( hid1_0, hid1_1, hid1_f0[1], hid1_f1[1])
-        sent = run(down_term, hids1, grads1, 1 - row)
-        got = swap(sent, "row")
-        down1_win = win(down1, 0)
-        gpre1_f0 = run(grad_pre_of, hid1_f0[0], dzf0, down1_win)
         down_a = run(lambda *a: plus(down_term, *a), hids1, grads1, row, got)
         down_a_moved = hop(down_a)
-        gpre1_f1 = run(grad_pre_of, hid1_f1[0], dzf1, down1_win)
-        acts1 = (xa0, xa1, xf0, xf1)
-        gpres1 = stack_win( gpre1_0, gpre1_1, gpre1_f0, gpre1_f1)
+        down_b = run(own_or, down_b, down_b_moved)
+        grad_down2 = join(down_b, 0)
+        gpre1_f0 = run(grad_pre_of, hid1_f0[0], dzf0, down1)
+        gpre1_f1 = run(grad_pre_of, hid1_f1[0], dzf1, down1)
+        acts1 = (xa0, xa1), (xf0, xf1)
+        gpres1 = (gpre1_0, gpre1_1), (gpre1_f0, gpre1_f1)
         sent = run(up_term, acts1, gpres1, 1 - row)
         got = swap(sent, "row")
-        ys1 = scatter_cols(run(dot, hid2_1, down2))
-        up_a = run(lambda *a: plus(up_term, *a), acts1, gpres1, row, got)
-        grad_up1 = join(up_a, 1)
-        down_a = run(lambda a, b: jnp.where(col == row, a, b), down_a, down_a_moved)
-        grad_down1 = join(down_a, 0)
-        grad_x = stack(add_round(dz0, xs0), add_round(dz1, xs1))
-        y_out = stack(add_round(z0, ys0), add_round(z1, ys1))
+        y0 = run(add_round, z0, ys0)
+        y1 = run(add_round, z1, ys1)
+        dx0 = run(add_round, dz0, xs0)
+        grad_up1 = run(lambda *a: plus(up_term, *a), acts1, gpres1, row, got)
+        dx1 = run(add_round, dz1, xs1)
+        grad_down1 = own_or(down_a, down_a_moved)
+        y_out = jnp.concatenate([y0, y1], axis=0)
+        grad_x = jnp.concatenate([dx0, dx1], axis=0)
         return y_out, grad_x, grad_up1, grad_down1, grad_up2, grad_down2
 
     return jax.shard_map(local_step, mesh=mesh, in_specs=(act_spec, weight_spec, weight_spec, weight_spec, weight_spec, act_spec), out_specs=(act_spec, act_spec, weight_spec, weight_spec, weight_spec, weight_spec), check_vma=False)

time: 2050 us -> 1680 us (0.82)
  waiting for transfers between devices: 793 us -> 347 us
  matrix products: 741 us -> 880 us
  starting transfers between devices: 147 us -> 88.9 us
  local copies, waits for them, and re-layouts: 70.2 us -> 47.8 us
    ppermute x20 -> x18, waiting for transfers between devices: 552 us -> 223 us  [swap(): return lax.ppermute(value, axis, [(0, 1), (1, 0)])]
    all_gather x8, waiting for transfers between devices: 239 us -> 124 us  [gather_cols(): return lax.all_gather(value, 'col', axis=1, tiled=True)]
    dot_general x32, matrix products: 247 us -> 359 us  [dot_first(): lax.dot_general(left_op, right_op, (((0,), (0,)), ((), ())), preferred_el...]
    ppermute x20 -> x18, starting transfers between devices: 130 us -> 70.6 us  [swap(): return lax.ppermute(value, axis, [(0, 1), (1, 0)])]
    add x4, other arithmetic: 56.9 us -> 82.2 us  [plus(): return fn(left, right, index) + received]
    dynamic_slice x8 -> x5, local copies, waits for them, and re-layouts: 44.2 us -> 24.8 us  [win(): return lax.dynamic_slice_in_dim(value, start, window, axis)]
  transfers between devices with their start and end apart: 41 -> 39, of which waited for: 16 -> 9; matrix products, arithmetic and copies ran while one was open for 46% -> 70% of each run, Pallas kernels for 0% -> 0%
where the time goes in v2:
time: 1680 us; the launch traced here: 1670 us
  matrix products  880 us (52%)
  waiting for transfers between devices  347 us (21%)
  other arithmetic  295 us (18%)
  starting transfers between devices  88.9 us (5%)
  local copies, waits for them, and re-layouts  47.8 us (3%)
    dot_general x32, matrix products, dot_first(): lax.dot_general(left_op, right_op, (((0,), (0,)), ((), ())), preferred_el...  359 us
    dot_general x12, matrix products, dot_last(): lax.dot_general(left_op, right_op, (((1,), (1,)), ((), ())), preferred_el...  276 us
    dot_general x12, matrix products, dot(): return jnp.dot(left_op, right_op, preferred_element_type=jnp.float32)  246 us
    ppermute x18, waiting for transfers between devices, swap(): return lax.ppermute(value, axis, [(0, 1), (1, 0)])  223 us
    all_gather x8, waiting for transfers between devices, gather_cols(): return lax.all_gather(value, 'col', axis=1, tiled=True)  124 us
    add x4, other arithmetic, plus(): return fn(left, right, index) + received  82.2 us
    ppermute x18, starting transfers between devices, swap(): return lax.ppermute(value, axis, [(0, 1), (1, 0)])  70.6 us
    convert_element_type x4, other arithmetic, grad_pre_of(): return gelu_grad(pre, dot_last(grad, down)).astype(jnp.bfloat16)  50 us
  transfers between devices with their start and end apart: 39, of which 9 were waited for; matrix products, arithmetic and copies ran while one was open for 70% of the time, Pallas kernels for 0%

profile of v2, /device:TPU:0, one launch (start us, length us, event | category | flops | bytes accessed | tf_op | source)
XLA Modules:
  0.0 1673.7 jit_solution(4083655858634648007)
XLA Ops:
  31.2 42.1 %all-gather.9.cloned.1.call-done = bf16[1024,1536]{1,0:T(8,128)(2,1)} async-done(((bf16[1024,768]{1,0:T(8,128)(2,1)}), bf16[1024,1536]{1,0:T(8,128)(2,1)}) %all-gather.9.cloned.1.call-update) | async-done | bytes 3145744 | tf_op jit(solution)/shard_map/all_gather | solution.py:39
  73.2 24.3 %fusion.49 = (bf16[1024,4480]{1,0:T(8,128)(2,1)}, f32[1024,4480]{1,0:T(8,128)}) fusion(bf16[1024,1536]{1,0:T(8,128)(2,1)} %all-gather.9.cloned.1.call-done, bf16[1536,4480]{1,0:T(8,128)(2,1)} %pad_maximum_fusion.1), kind=kOutput, calls=%fused_computation.67 | convolution fusion | flops 14134149120 | bytes 44433408 | tf_op jit(solution)/shard_map/dot_general | solution.py:18
  97.6 36.3 %all-gather.11.cloned.1.call-done = bf16[1024,1536]{1,0:T(8,128)(2,1)} async-done(((bf16[1024,768]{1,0:T(8,128)(2,1)}), bf16[1024,1536]{1,0:T(8,128)(2,1)}) %all-gather.11.cloned.1.call-update) | async-done | bytes 3145744 | tf_op jit(solution)/shard_map/all_gather | solution.py:39
  133.9 24.5 %fusion.57 = (bf16[1024,4480]{1,0:T(8,128)(2,1)}, f32[1024,4480]{1,0:T(8,128)}) fusion(bf16[1024,1536]{1,0:T(8,128)(2,1)} %all-gather.11.cloned.1.call-done, bf16[1536,4480]{1,0:T(8,128)(2,1)} %pad_maximum_fusion.1), kind=kOutput, calls=%fused_computation.75 | convolution fusion | flops 14134149120 | bytes 44433408 | tf_op jit(solution)/shard_map/dot_general | solution.py:18
  204.7 21.9 %fusion.216 = f32[1024,1536]{1,0:T(8,128)} fusion(bf16[1024,4480]{1,0:T(8,128)(2,1)} %get-tuple-element.303, bf16[4480,1536]{1,0:T(8,128)(2,1)} %copy-done.10), kind=kOutput, calls=%fused_computation.290 | convolution fusion | flops 14092861440 | bytes 29229056 | tf_op jit(solution)/shard_map/dot_general | solution.py:18
  254.0 53.1 %collective-permute-done.3 = bf16[1024,1536]{1,0:T(8,128)(2,1)S(1)} collective-permute-done((bf16[1024,1536]{1,0:T(8,128)(2,1)}, bf16[1024,1536]{1,0:T(8,128)(2,1)S(1)}, u32[]{:S(2)}, u32[]{:S(2)}) %collective-permute-start.3) | collective-permute-done | bytes 3145760 | tf_op jit(solution)/shard_map/ppermute | solution.py:30
  332.7 42.0 %collective-permute-done.7 = bf16[1024,1536]{1,0:T(8,128)(2,1)} collective-permute-done((bf16[1024,1536]{1,0:T(8,128)(2,1)}, bf16[1024,1536]{1,0:T(8,128)(2,1)}, u32[]{:S(2)}, u32[]{:S(2)}) %collective-permute-start.7) | collective-permute-done | bytes 3145760 | tf_op jit(solution)/shard_map/ppermute | solution.py:30
  374.7 24.5 %fusion.73 = (bf16[1024,4480]{1,0:T(8,128)(2,1)}, f32[1024,4480]{1,0:T(8,128)}) fusion(bf16[1024,1536]{1,0:T(8,128)(2,1)} %collective-permute-done.7, bf16[1536,4480]{1,0:T(8,128)(2,1)} %pad_maximum_fusion.1), kind=kOutput, calls=%fused_computation.91 | convolution fusion | flops 14134149120 | bytes 44433408 | tf_op jit(solution)/shard_map/dot_general | solution.py:18
  430.9 41.1 %all-gather.13.cloned.1.call-done = bf16[1024,1536]{1,0:T(8,128)(2,1)} async-done(((bf16[1024,768]{1,0:T(8,128)(2,1)}), bf16[1024,1536]{1,0:T(8,128)(2,1)}) %all-gather.13.cloned.1.call-update) | async-done | bytes 3145744 | tf_op jit(solution)/shard_map/all_gather | solution.py:39
  514.1 30.3 %fusion.6 = bf16[1024,4480]{1,0:T(8,128)(2,1)} fusion(f32[1024,4480]{1,0:T(8,128)} %get-tuple-element.210, bf16[1024,1536]{1,0:T(8,128)(2,1)S(1)} %copy-done.17, bf16[4480,1536]{1,0:T(8,128)(2,1)} %pad_maximum_fusion), kind=kOutput, calls=%fused_computation.24 | convolution fusion | flops 14184611840 | bytes 44433408 | tf_op jit(solution)/shard_map/dot_general | solution.py:22
  544.6 21.9 %fusion.217 = f32[1024,1536]{1,0:T(8,128)} fusion(bf16[1024,4480]{1,0:T(8,128)(2,1)} %fusion.6, bf16[1536,4480]{1,0:T(8,128)(2,1)} %pad_maximum_fusion.3), kind=kOutput, calls=%fused_computation.291 | convolution fusion | flops 14092861440 | bytes 29229056 | tf_op jit(solution)/shard_map/dot_general | solution.py:22
  566.6 23.4 %fusion.89 = (bf16[1024,4480]{1,0:T(8,128)(2,1)}, f32[1024,4480]{1,0:T(8,128)}) fusion(bf16[1024,1536]{1,0:T(8,128)(2,1)S(1)} %copy-done.22, bf16[1536,4480]{1,0:T(8,128)(2,1)} %pad_maximum_fusion.3), kind=kOutput, calls=%fused_computation.107 | convolution fusion | flops 14134149120 | bytes 44433408 | tf_op jit(solution)/shard_map/dot_general | solution.py:18
  590.0 31.5 %fusion.13 = bf16[1024,4480]{1,0:T(8,128)(2,1)} fusion(f32[1024,4480]{1,0:T(8,128)} %get-tuple-element.218, bf16[1024,1536]{1,0:T(8,128)(2,1)} %all-gather.19.cloned.1.call-done, bf16[4480,1536]{1,0:T(8,128)(2,1)} %pad_maximum_fusion), kind=kOutput, calls=%fused_computation.31 | convolution fusion | flops 14184611840 | bytes 44433408 | tf_op jit(solution)/shard_map/dot_general | solution.py:22
  621.5 22.2 %fusion.218 = f32[1024,1536]{1,0:T(8,128)} fusion(bf16[1024,4480]{1,0:T(8,128)(2,1)} %fusion.13, bf16[1536,4480]{1,0:T(8,128)(2,1)} %pad_maximum_fusion.3), kind=kOutput, calls=%fused_computation.292 | convolution fusion | flops 14092861440 | bytes 29229056 | tf_op jit(solution)/shard_map/dot_general | solution.py:22
  953.9 31.9 %fusion.20 = bf16[1024,4480]{1,0:T(8,128)(2,1)} fusion(f32[1024,4480]{1,0:T(8,128)} %get-tuple-element.282, bf16[1024,1536]{1,0:T(8,128)(2,1)} %all-gather.21.cloned.1.call-done, bf16[4480,1536]{1,0:T(8,128)(2,1)} %copy-done.10), kind=kOutput, calls=%fused_computation.38 | convolution fusion | flops 14184611840 | bytes 44433408 | tf_op jit(solution)/shard_map/dot_general | solution.py:22
  985.8 21.7 %fusion.223 = f32[1024,1536]{1,0:T(8,128)} fusion(bf16[1024,4480]{1,0:T(8,128)(2,1)} %fusion.20, bf16[1536,4480]{1,0:T(8,128)(2,1)} %pad_maximum_fusion.1), kind=kOutput, calls=%fused_computation.297 | convolution fusion | flops 14092861440 | bytes 29229056 | tf_op jit(solution)/shard_map/dot_general | solution.py:22
  1007.5 30.2 %fusion.27 = bf16[1024,4480]{1,0:T(8,128)(2,1)} fusion(f32[1024,4480]{1,0:T(8,128)} %get-tuple-element.287, bf16[1024,1536]{1,0:T(8,128)(2,1)S(1)} %copy-done.24, bf16[4480,1536]{1,0:T(8,128)(2,1)} %copy-done.10), kind=kOutput, calls=%fused_computation.45 | convolution fusion | flops 14184611840 | bytes 44433408 | tf_op jit(solution)/shard_map/dot_general | solution.py:22
  1078.3 25.2 %add_add_fusion.3 = f32[4480,768]{1,0:T(8,128)} fusion(f32[4480,768]{1,0:T(8,128)} %fusion.144, f32[4480,768]{1,0:T(8,128)} %fusion.149, f32[4480,768]{1,0:T(8,128)} %fusion.147, bf16[1024,4480]{1,0:T(8,128)(2,1)} %get-tuple-element.305, bf16[1024,1536]{1,0:T(8,128)(2,1)} %collective-permute-done.15, s32[]{:T(128)S(6)} %select_n.180), kind=kOutput, calls=%fused_computation.121 | convolution fusion | flops 7056752640 | bytes 65798148 | tf_op jit(solution)/shard_map/dot_general | solution.py:26
  1107.1 22.0 %fusion.224 = f32[1024,1536]{1,0:T(8,128)} fusion(bf16[1024,4480]{1,0:T(8,128)(2,1)} %fusion.27, bf16[1536,4480]{1,0:T(8,128)(2,1)} %pad_maximum_fusion.1), kind=kOutput, calls=%fused_computation.298 | convolution fusion | flops 14092861440 | bytes 29229056 | tf_op jit(solution)/shard_map/dot_general | solution.py:22
  1181.4 27.8 %add_add_fusion.2 = f32[4480,768]{1,0:T(8,128)} fusion(f32[4480,768]{1,0:T(8,128)} %collective-permute-done.18, f32[4480,768]{1,0:T(8,128)} %fusion.138, f32[4480,768]{1,0:T(8,128)} %fusion.136, f32[4480,768]{1,0:T(8,128)} %fusion.142, f32[4480,768]{1,0:T(8,128)} %fusion.140), kind=kLoop, calls=%fused_computation.120 | loop fusion | flops 13762560 | bytes 82575360 | tf_op jit(solution)/shard_map/add | solution.py:126
  1325.9 25.4 %add_add_fusion.1 = f32[768,4480]{1,0:T(8,128)} fusion(f32[768,4480]{1,0:T(8,128)} %fusion.129, f32[768,4480]{1,0:T(8,128)} %fusion.134, f32[768,4480]{1,0:T(8,128)} %fusion.132, bf16[1024,4480]{1,0:T(8,128)(2,1)} %fusion.34, bf16[1024,1536]{1,0:T(8,128)(2,1)S(1)} %copy-done.13, s32[]{:T(128)S(6)} %select_n.183), kind=kOutput, calls=%fused_computation.119 | convolution fusion | flops 7056752640 | bytes 65798148 | tf_op jit(solution)/shard_map/dot_general | solution.py:26
  1351.3 46.6 %collective-permute-start.19 = (f32[768,4480]{1,0:T(8,128)}, f32[768,4480]{1,0:T(8,128)}, u32[]{:S(2)}, u32[]{:S(2)}) collective-permute-start(f32[768,4480]{1,0:T(8,128)} %add_add_fusion.1), channel_id=1, source_target_pairs={{0,1},{1,0},{2,3},{3,2},{4,5},{5,4},{6,7},{7,6}} | collective-permute-start | bytes 41287688 | tf_op jit(solution)/shard_map/ppermute | solution.py:30
  1439.4 113.1 %collective-permute-done.22 = f32[2304,768]{1,0:T(8,128)} collective-permute-done((f32[2304,768]{1,0:T(8,128)}, f32[2304,768]{1,0:T(8,128)}, u32[]{:S(2)}, u32[]{:S(2)}) %collective-permute-start.22) | collective-permute-done | bytes 7077920 | tf_op jit(solution)/shard_map/ppermute | solution.py:30
  1621.6 27.1 %add_add_fusion = f32[768,4480]{1,0:T(8,128)} fusion(f32[768,4480]{1,0:T(8,128)} %collective-permute-done.19, f32[768,4480]{1,0:T(8,128)} %fusion.123, f32[768,4480]{1,0:T(8,128)} %fusion.121, f32[768,4480]{1,0:T(8,128)} %fusion.127, f32[768,4480]{1,0:T(8,128)} %fusion.125), kind=kLoop, calls=%fused_computation.118 | loop fusion | flops 13762560 | bytes 82575360 | tf_op jit(solution)/shard_map/add | solution.py:126
  (403 shorter events, 848.1 us)
Async XLA Ops:
  11.9 146.5 %collective-permute-start.1 = (bf16[4480,768]{1,0:T(8,128)(2,1)}, bf16[4480,768]{1,0:T(8,128)(2,1)}, u32[]{:S(2)}, u32[]{:S(2)}) collective-permute-start(bf16[4480,768]{1,0:T(8,128)(2,1)} %param.8), channel_id=1, source_target_pairs={{1,2},{2,1},{5,6},{6,5}} | collective-permute-start | bytes 20643848 | tf_op jit(solution)/shard_map/ppermute | solution.py:98
  15.4 313.8 %reduce-scatter.9.cloned.1.call-start = ((), (), s32[]{:S(2)}) async-start(), calls=%async_computation.10 | async-start | bytes 9437184 | tf_op jit(solution)/shard_map/reduce_scatter | solution.py:43
  204.6 221.1 %reduce-scatter.11.cloned.1.call-start = ((), (), s32[]{:S(2)}) async-start(), calls=%async_computation.12 | async-start | bytes 9437184 | tf_op jit(solution)/shard_map/reduce_scatter | solution.py:43
  226.6 202.6 %all-gather.17.cloned.1.call-start = ((), (), s32[]{:S(2)}) async-start(), calls=%async_computation.14 | async-start | bytes 4718592 | tf_op jit(solution)/shard_map/all_gather | solution.py:39
  235.4 236.5 %all-gather.13.cloned.1.call-start = ((), (), s32[]{:S(2)}) async-start(), calls=%async_computation.11 | async-start | bytes 4718592 | tf_op jit(solution)/shard_map/all_gather | solution.py:39
  238.1 136.6 %collective-permute-start.7 = (bf16[1024,1536]{1,0:T(8,128)(2,1)}, bf16[1024,1536]{1,0:T(8,128)(2,1)}, u32[]{:S(2)}, u32[]{:S(2)}) collective-permute-start(bf16[1024,1536]{1,0:T(8,128)(2,1)} %all-gather.11.cloned.1.call-done), channel_id=1, source_target_pairs={{0,4},{4,0},{1,5},{5,1},{2,6},{6,2},{3,7},{7,3}} | collective-permute-start | bytes 9437192 | tf_op jit(solution)/shard_map/ppermute | solution.py:30
  238.1 161.0 %collective-permute-start.6 = (bf16[2240,768]{1,0:T(8,128)(2,1)}, bf16[2240,768]{1,0:T(8,128)(2,1)}, u32[]{:S(2)}, u32[]{:S(2)}) collective-permute-start(bf16[2240,768]{1,0:T(8,128)(2,1)} %collective-permute-done.5), channel_id=1, source_target_pairs={{1,5},{5,1},{2,6},{6,2}} | collective-permute-start | bytes 10321928 | tf_op jit(solution)/shard_map/ppermute | solution.py:102
  429.2 160.8 %all-gather.19.cloned.1.call-start = ((), (), s32[]{:S(2)}) async-start(), calls=%async_computation.15 | async-start | bytes 4718592 | tf_op jit(solution)/shard_map/all_gather | solution.py:39
  429.3 269.8 %collective-permute-start.11 = (bf16[1024,1536]{1,0:T(8,128)(2,1)}, bf16[1024,1536]{1,0:T(8,128)(2,1)}, u32[]{:S(2)}, u32[]{:S(2)}) collective-permute-start(bf16[1024,1536]{1,0:T(8,128)(2,1)} %all-gather.17.cloned.1.call-done), channel_id=1, source_target_pairs={{0,4},{4,0},{1,5},{5,1},{2,6},{6,2},{3,7},{7,3}} | collective-permute-start | bytes 9437192 | tf_op jit(solution)/shard_map/ppermute | solution.py:30
  430.8 264.8 %reduce-scatter.13.cloned.1.call-start = ((), (), s32[]{:S(2)}) async-start(), calls=%async_computation.16 | async-start | bytes 9437184 | tf_op jit(solution)/shard_map/reduce_scatter | solution.py:43
  472.0 178.2 %collective-permute-start.9 = (bf16[1024,1536]{1,0:T(8,128)(2,1)}, bf16[1024,1536]{1,0:T(8,128)(2,1)}, u32[]{:S(2)}, u32[]{:S(2)}) collective-permute-start(bf16[1024,1536]{1,0:T(8,128)(2,1)} %all-gather.13.cloned.1.call-done), channel_id=1, source_target_pairs={{0,4},{4,0},{1,5},{5,1},{2,6},{6,2},{3,7},{7,3}} | collective-permute-start | bytes 9437192 | tf_op jit(solution)/shard_map/ppermute | solution.py:30
  544.4 138.1 %collective-permute-start.10 = (bf16[1024,1536]{1,0:T(8,128)(2,1)}, bf16[1024,1536]{1,0:T(8,128)(2,1)}, u32[]{:S(2)}, u32[]{:S(2)}) collective-permute-start(bf16[1024,1536]{1,0:T(8,128)(2,1)} %all-gather.15.cloned.1.call-done), channel_id=1, source_target_pairs={{0,4},{4,0},{1,5},{5,1},{2,6},{6,2},{3,7},{7,3}} | collective-permute-start | bytes 9437192 | tf_op jit(solution)/shard_map/ppermute | solution.py:30
  566.5 209.7 %reduce-scatter.15.cloned.1.call-start = ((), (), s32[]{:S(2)}) async-start(), calls=%async_computation.17 | async-start | bytes 9437184 | tf_op jit(solution)/shard_map/reduce_scatter | solution.py:43
  658.2 202.0 %all-gather.23.cloned.1.call-start = ((), (), s32[]{:S(2)}) async-start(), calls=%async_computation.20 | async-start | bytes 4718592 | tf_op jit(solution)/shard_map/all_gather | solution.py:39
  790.3 638.2 %reduce-scatter.17.cloned.1.call-start = ((), (), s32[]{:S(2)}) async-start(), calls=%async_computation.18 | async-start | bytes 9437184 | tf_op jit(solution)/shard_map/reduce_scatter | solution.py:43
  860.2 177.5 %collective-permute-start.17 = (bf16[1024,1536]{1,0:T(8,128)(2,1)}, bf16[1024,1536]{1,0:T(8,128)(2,1)}, u32[]{:S(2)}, u32[]{:S(2)}) collective-permute-start(bf16[1024,1536]{1,0:T(8,128)(2,1)} %all-gather.23.cloned.1.call-done), channel_id=1, source_target_pairs={{0,4},{4,0},{1,5},{5,1},{2,6},{6,2},{3,7},{7,3}} | collective-permute-start | bytes 9437192 | tf_op jit(solution)/shard_map/ppermute | solution.py:30
  864.5 173.2 %collective-permute-start.15 = (bf16[1024,1536]{1,0:T(8,128)(2,1)}, bf16[1024,1536]{1,0:T(8,128)(2,1)}, u32[]{:S(2)}, u32[]{:S(2)}) collective-permute-start(bf16[1024,1536]{1,0:T(8,128)(2,1)} %all-gather.21.cloned.1.call-done), channel_id=1, source_target_pairs={{0,4},{4,0},{1,5},{5,1},{2,6},{6,2},{3,7},{7,3}} | collective-permute-start | bytes 9437192 | tf_op jit(solution)/shard_map/ppermute | solution.py:30
  887.6 544.3 %reduce-scatter.19.cloned.1.call-start = ((), (), s32[]{:S(2)}) async-start(), calls=%async_computation.21 | async-start | bytes 9437184 | tf_op jit(solution)/shard_map/reduce_scatter | solution.py:43
  1037.7 397.7 %reduce-scatter.21.cloned.1.call-start = ((), (), s32[]{:S(2)}) async-start(), calls=%async_computation.22 | async-start | bytes 9437184 | tf_op jit(solution)/shard_map/reduce_scatter | solution.py:43
  1103.5 296.2 %collective-permute-start.21 = (f32[768,2304]{1,0:T(8,128)}, f32[768,2304]{1,0:T(8,128)}, u32[]{:S(2)}, u32[]{:S(2)}) collective-permute-start(f32[768,2304]{1,0:T(8,128)} %add_add_fusion.6), channel_id=1, source_target_pairs={{0,4},{4,0},{1,5},{5,1},{2,6},{6,2},{3,7},{7,3}} | collective-permute-start | bytes 21233672 | tf_op jit(solution)/shard_map/ppermute | solution.py:30
  1107.1 541.6 %reduce-scatter.23.cloned.1.call-start = ((), (), s32[]{:S(2)}) async-start(), calls=%async_computation.23 | async-start | bytes 9437184 | tf_op jit(solution)/shard_map/reduce_scatter | solution.py:43
  1351.3 219.7 %collective-permute-start.19 = (f32[768,4480]{1,0:T(8,128)}, f32[768,4480]{1,0:T(8,128)}, u32[]{:S(2)}, u32[]{:S(2)}) collective-permute-start(f32[768,4480]{1,0:T(8,128)} %add_add_fusion.1), channel_id=1, source_target_pairs={{0,1},{1,0},{2,3},{3,2},{4,5},{5,4},{6,7},{7,6}} | collective-permute-start | bytes 41287688 | tf_op jit(solution)/shard_map/ppermute | solution.py:30
  1397.9 154.6 %collective-permute-start.22 = (f32[2304,768]{1,0:T(8,128)}, f32[2304,768]{1,0:T(8,128)}, u32[]{:S(2)}, u32[]{:S(2)}) collective-permute-start(f32[2304,768]{1,0:T(8,128)} %broadcast_select_fusion.12), channel_id=1, source_target_pairs={{0,4},{4,0},{1,5},{5,1},{2,6},{6,2},{3,7},{7,3}} | collective-permute-start | bytes 21233672 | tf_op jit(solution)/shard_map/ppermute | solution.py:30
  1423.0 232.4 %collective-permute-start.20 = (f32[4480,768]{1,0:T(8,128)}, f32[4480,768]{1,0:T(8,128)}, u32[]{:S(2)}, u32[]{:S(2)}) collective-permute-start(f32[4480,768]{1,0:T(8,128)} %add_add_fusion.2), channel_id=1, source_target_pairs={{1,2},{2,1},{5,6},{6,5}} | collective-permute-start | bytes 41287688 | tf_op jit(solution)/shard_map/ppermute | solution.py:98
  (117 other events, 2896.4 us)
Sparse Core Ops, SparseCore 0:
  12.0 61.2 all-gather.8
  74.7 59.0 all-gather.10
  204.8 97.9 reduce-scatter.8
  304.9 79.9 reduce-scatter.10
  386.3 42.1 all-gather.16
  429.8 42.1 all-gather.12
  474.0 42.1 all-gather.14
  517.7 42.1 all-gather.18
  566.7 74.4 reduce-scatter.12
  658.3 73.3 reduce-scatter.14
  779.8 41.1 all-gather.22
  822.4 42.1 all-gather.20
  887.7 73.4 reduce-scatter.16
  1037.9 73.0 reduce-scatter.18
  1113.0 108.5 reduce-scatter.20
  1399.8 95.0 reduce-scatter.22

commit v3 on v2

--- a/solution.py
+++ b/solution.py
@@ -1,6 +1,8 @@
 import jax
 import jax.numpy as jnp
 from jax import lax
+from jax.experimental import pallas as pl
+from jax.experimental.pallas import tpu as pltpu
 from jax.sharding import PartitionSpec as P
 
 LANES = 128
@@ -51,11 +53,11 @@
 
 def hidden_of(acts, up):
     pre = dot(acts, up)
-    return pre, gelu_tanh(pre).astype(jnp.bfloat16)
-
-
-def grad_pre_of(pre, grad, down):
-    return gelu_grad(pre, dot_last(grad, down)).astype(jnp.bfloat16)
+    return gelu_grad(pre, jnp.ones_like(pre)), gelu_tanh(pre).astype(jnp.bfloat16)
+
+
+def grad_pre_of(slope, grad, down):
+    return (dot_last(grad, down) * slope).astype(jnp.bfloat16)
 
 
 def add_round(base, total):
@@ -64,6 +66,46 @@
 
 def after(value, *others):
     return lax.optimization_barrier((value, *others))[0]
+
+
+def token_sum_kernel(index_ref, *refs):
+    lefts, rights, rest = refs[:4], refs[4:8], refs[8:]
+    terms = [dot_first(left[...], right[...]) for left, right in zip(lefts, rights)]
+    total = (terms[0] + terms[1]) + (terms[2] + terms[3])
+    out = rest[-1]
+    if len(rest) == 2:
+        total = total + rest[0][...]
+    out[...] = total
+
+
+def tile_of(size):
+    return max(t for t in range(LANES, 897, LANES) if size % t == 0)
+
+
+def token_sum(lefts, rights, index, received, halves_left):
+    depth = lefts[0].shape[0]
+    whole, halved = (rights, lefts) if halves_left else (lefts, rights)
+    size, half = whole[0].shape[1], halved[0].shape[1] // 2
+    tile = tile_of(size)
+    whole_spec = pl.BlockSpec((depth, tile), lambda j, s: (0, j))
+    half_spec = pl.BlockSpec((depth, half), lambda j, s: (0, s[0]))
+    if halves_left:
+        shape, out_spec = (half, size), pl.BlockSpec((half, tile), lambda j, s: (0, j))
+        specs = [half_spec] * 4 + [whole_spec] * 4
+    else:
+        shape, out_spec = (size, half), pl.BlockSpec((tile, half), lambda j, s: (j, 0))
+        specs = [whole_spec] * 4 + [half_spec] * 4
+    specs = specs + [out_spec] * len(received)
+    flops = 2 * 4 * depth * size * half
+    moved = 4 * depth * (size + half) * 2 + (1 + len(received)) * size * half * 4
+    return pl.pallas_call(
+        token_sum_kernel,
+        out_shape=jax.ShapeDtypeStruct(shape, jnp.float32),
+        grid_spec=pltpu.PrefetchScalarGridSpec(num_scalar_prefetch=1, grid=(size // tile,), in_specs=specs, out_specs=out_spec),
+        compiler_params=pltpu.CompilerParams(vmem_limit_bytes=60 * 1024 * 1024, dimension_semantics=("arbitrary",)),
+        cost_estimate=pl.CostEstimate(flops=flops, bytes_accessed=moved, transcendentals=0),
+        name="token_sum_up" if halves_left else "token_sum_down",
+    )(jnp.reshape(index, (1,)).astype(jnp.int32), *lefts, *rights, *received)
 
 
 def solution(mesh):
@@ -114,16 +156,11 @@
             high = lax.slice_in_dim(high, skip, window, axis=axis)
             return jnp.concatenate([low, high], axis=axis)
 
-        def down_term(hids, grads, index):
-            near, far = ([dot_first(h, half_of(g, index, 1)) for h, g in zip(*p)] for p in zip(hids, grads))
-            return (near[0] + near[1]) + (far[0] + far[1])
-
-        def up_term(acts, gpres, index):
-            near, far = ([dot_first(half_of(a, index, 1), g) for a, g in zip(*p)] for p in zip(acts, gpres))
-            return (near[0] + near[1]) + (far[0] + far[1])
-
-        def plus(fn, left, right, index, received):
-            return fn(left, right, index) + received
+        def down_term(hids, grads, index, *received):
+            return token_sum(hids[0] + hids[1], grads[0] + grads[1], index, received, False)
+
+        def up_term(acts, gpres, index, *received):
+            return token_sum(acts[0] + acts[1], gpres[0] + gpres[1], index, received, True)
 
         x0, x1 = split(tokens)
         g0, g1 = split(grad_out)
@@ -187,20 +224,20 @@
         got = swap(sent, "row")
         dz1 = run(add_round, g1, ds1)
         dza1 = gather_cols(dz1)
-        dzf0 = swap(dza0, "dep")
-        up_b = run(lambda *a: plus(up_term, *a), acts2, gpres2, row, got)
-        dzf1 = swap(dza1, "dep")
+        up_b = run(up_term, acts2, gpres2, row, got)
         hids2 = (win(hid2_0, 1), win(hid2_1, 1)), (hid2_f0, hid2_f1)
         grads2 = (ga0, ga1), (gf0, gf1)
         sent = run(down_term, hids2, grads2, 1 - row)
         got = swap(sent, "row")
-        grad_up2 = join(after(up_b, sent), 1)
+        dzf0 = swap(dza0, "dep")
         ys0 = scatter_cols(run(dot, hid2_0, down2))
-        down_b = run(lambda *a: plus(down_term, *a), hids2, grads2, row, got)
+        down_b = run(down_term, hids2, grads2, row, got)
+        dzf1 = swap(after(dza1, down_b), "dep")
         down_b_moved = hop(after(down_b, dza1))
         ys1 = scatter_cols(run(dot, hid2_1, down2))
 
         gpre1_0 = run(grad_pre_of, pre1_0, dza0, down1)
+        grad_up2 = join(after(up_b, gpre1_0), 1)
         xs0 = scatter_cols(run(dot_last, gpre1_0, up1))
         gpre1_1 = run(grad_pre_of, pre1_1, dza1, down1)
         grads1 = (dza0, dza1), (dzf0, dzf1)
@@ -208,7 +245,7 @@
         sent = run(down_term, hids1, grads1, 1 - row)
         got = swap(sent, "row")
         xs1 = scatter_cols(run(dot_last, gpre1_1, up1))
-        down_a = run(lambda *a: plus(down_term, *a), hids1, grads1, row, got)
+        down_a = run(down_term, hids1, grads1, row, got)
         down_a_moved = hop(down_a)
         down_b = run(own_or, down_b, down_b_moved)
         grad_down2 = join(down_b, 0)
@@ -221,7 +258,7 @@
         y0 = run(add_round, z0, ys0)
         y1 = run(add_round, z1, ys1)
         dx0 = run(add_round, dz0, xs0)
-        grad_up1 = run(lambda *a: plus(up_term, *a), acts1, gpres1, row, got)
+        grad_up1 = run(up_term, acts1, gpres1, row, got)
         dx1 = run(add_round, dz1, xs1)
         grad_down1 = own_or(down_a, down_a_moved)
         y_out = jnp.concatenate([y0, y1], axis=0)

time: 1680 us -> 1550 us (0.923)
  matrix products: 880 us -> 576 us
  Pallas kernels: 0 us -> 250 us
  other arithmetic: 295 us -> 159 us
  waiting for transfers between devices: 347 us -> 379 us
  starting transfers between devices: 88.9 us -> 114 us
    dot_general x32 -> x0, matrix products: 359 us -> none  [dot_first(): lax.dot_general(left_op, right_op, (((0,), (0,)), ((), ())), preferred_el...]
    pallas_call x0 -> x8, Pallas kernels: none -> 250 us  [token_sum(): pl.pallas_call(token_sum_kernel, out_shape=jax.ShapeDtypeStruct(shape, jn...]
    add x4 -> x0, other arithmetic: 82.2 us -> none  [plus(): return fn(left, right, index) + received]
    dot_general x12, matrix products: 246 us -> 298 us  [dot(): return jnp.dot(left_op, right_op, preferred_element_type=jnp.float32)]
    convert_element_type x4 -> x0, other arithmetic: 50 us -> none  [grad_pre_of(): return gelu_grad(pre, dot_last(grad, down)).astype(jnp.bfloat16)]
    ppermute x18, waiting for transfers between devices: 223 us -> 270 us  [swap(): return lax.ppermute(value, axis, [(0, 1), (1, 0)])]
    ppermute x18, starting transfers between devices: 70.6 us -> 96.1 us  [swap(): return lax.ppermute(value, axis, [(0, 1), (1, 0)])]
  transfers between devices with their start and end apart: 39 -> 39, of which waited for: 9 -> 8; matrix products, arithmetic and copies ran while one was open for 70% -> 47% of each run, Pallas kernels for 0% -> 16%
where the time goes in v3:
time: 1550 us; the launch traced here: 1540 us
  matrix products  576 us (37%)
  waiting for transfers between devices  379 us (24%)
  Pallas kernels  250 us (16%)
  other arithmetic  159 us (10%)
  starting transfers between devices  114 us (7%)
  local copies, waits for them, and re-layouts  50.1 us (3%)
    dot_general x12, matrix products, dot(): return jnp.dot(left_op, right_op, preferred_element_type=jnp.float32)  298 us
    dot_general x12, matrix products, dot_last(): lax.dot_general(left_op, right_op, (((1,), (1,)), ((), ())), preferred_el...  278 us
    ppermute x18, waiting for transfers between devices, swap(): return lax.ppermute(value, axis, [(0, 1), (1, 0)])  270 us
    pallas_call x8, Pallas kernels, token_sum(): pl.pallas_call(token_sum_kernel, out_shape=jax.ShapeDtypeStruct(shape, jn...  250 us
    all_gather x8, waiting for transfers between devices, gather_cols(): return lax.all_gather(value, 'col', axis=1, tiled=True)  109 us
    ppermute x18, starting transfers between devices, swap(): return lax.ppermute(value, axis, [(0, 1), (1, 0)])  96.1 us
    select_n x4, other arithmetic, own_or(): return jnp.where(col == row, shard, moved)  34.3 us
    select_n x5, other arithmetic, in_order(): low = jnp.where(index == 0, mine, other)  32.2 us
  transfers between devices with their start and end apart: 39, of which 8 were waited for; matrix products, arithmetic and copies ran while one was open for 47% of the time, Pallas kernels for 16%

profile of v3, /device:TPU:0, one launch (start us, length us, event | category | flops | bytes accessed | tf_op | source)
XLA Modules:
  0.0 1543.2 jit_solution(12941317227715167972)
XLA Ops:
  31.2 42.1 %all-gather.9.cloned.1.call-done.refs_0_ = bf16[1024,1536]{1,0:T(8,128)(2,1)} async-done(((bf16[1024,768]{1,0:T(8,128)(2,1)}), bf16[1024,1536]{1,0:T(8,128)(2,1)}) %all-gather.9.cloned.1.call-update) | async-done | bytes 3145744 | tf_op jit(solution)/shard_map/all_gather | solution.py:41
  73.3 31.1 %fusion.5 = (f32[1024,4480]{1,0:T(8,128)}, bf16[1024,4480]{1,0:T(8,128)(2,1)}) fusion(bf16[1024,1536]{1,0:T(8,128)(2,1)} %all-gather.9.cloned.1.call-done.refs_0_, bf16[1536,4480]{1,0:T(8,128)(2,1)} %pad_maximum_fusion.1), kind=kOutput, calls=%fused_computation.17 | convolution fusion | flops 14180024320 | bytes 44433408 | tf_op jit(solution)/shard_map/dot_general | solution.py:20
  104.4 29.6 %all-gather.11.cloned.1.call-done.refs_1_ = bf16[1024,1536]{1,0:T(8,128)(2,1)} async-done(((bf16[1024,768]{1,0:T(8,128)(2,1)}), bf16[1024,1536]{1,0:T(8,128)(2,1)}) %all-gather.11.cloned.1.call-update) | async-done | bytes 3145744 | tf_op jit(solution)/shard_map/all_gather | solution.py:41
  134.0 31.2 %fusion.11 = (f32[1024,4480]{1,0:T(8,128)}, bf16[1024,4480]{1,0:T(8,128)(2,1)}) fusion(bf16[1024,1536]{1,0:T(8,128)(2,1)} %all-gather.11.cloned.1.call-done.refs_1_, bf16[1536,4480]{1,0:T(8,128)(2,1)} %pad_maximum_fusion.1), kind=kOutput, calls=%fused_computation.23 | convolution fusion | flops 14180024320 | bytes 44433408 | tf_op jit(solution)/shard_map/dot_general | solution.py:20
  260.5 120.6 %collective-permute-done.3.refs_2_ = bf16[1024,1536]{1,0:T(8,128)(2,1)S(1)} collective-permute-done((bf16[1024,1536]{1,0:T(8,128)(2,1)}, bf16[1024,1536]{1,0:T(8,128)(2,1)S(1)}, u32[]{:S(2)}, u32[]{:S(2)}) %collective-permute-start.3) | collective-permute-done | bytes 3145760 | tf_op jit(solution)/shard_map/ppermute | solution.py:32
  382.8 26.8 %fusion.17 = (f32[1024,4480]{1,0:T(8,128)}, bf16[1024,4480]{1,0:T(8,128)(2,1)}) fusion(bf16[1024,1536]{1,0:T(8,128)(2,1)S(1)} %collective-permute-done.3.refs_2_, bf16[1536,4480]{1,0:T(8,128)(2,1)S(1)} %bitcast.63), kind=kOutput, calls=%fused_computation.29 | convolution fusion | flops 14180024320 | bytes 44433408 | tf_op jit(solution)/shard_map/dot_general | solution.py:20
  413.0 31.2 %fusion.23 = (f32[1024,4480]{1,0:T(8,128)}, bf16[1024,4480]{1,0:T(8,128)(2,1)}) fusion(bf16[1024,1536]{1,0:T(8,128)(2,1)} %collective-permute-done.7.refs_3_, bf16[1536,4480]{1,0:T(8,128)(2,1)} %pad_maximum_fusion.1), kind=kOutput, calls=%fused_computation.35 | convolution fusion | flops 14180024320 | bytes 44433408 | tf_op jit(solution)/shard_map/dot_general | solution.py:20
  465.1 37.3 %all-gather.13.cloned.1.call-done.refs_0_ = bf16[1024,1536]{1,0:T(8,128)(2,1)} async-done(((bf16[1024,768]{1,0:T(8,128)(2,1)}), bf16[1024,1536]{1,0:T(8,128)(2,1)}) %all-gather.13.cloned.1.call-update) | async-done | bytes 3145744 | tf_op jit(solution)/shard_map/all_gather | solution.py:41
  523.7 27.2 %multiply_convert_fusion.7 = (bf16[1024,4480]{1,0:T(8,128)(2,1)}, f32[1024,4480]{1,0:T(8,128)}) fusion(bf16[1024,1536]{1,0:T(8,128)(2,1)S(1)} %copy-done.13, bf16[1536,4480]{1,0:T(8,128)(2,1)S(1)} %bitcast.59), kind=kOutput, calls=%fused_computation.55 | convolution fusion | flops 14180024320 | bytes 44433408 | tf_op jit(solution)/shard_map/dot_general | solution.py:20
  550.9 30.1 %multiply_convert_fusion.6 = bf16[1024,4480]{1,0:T(8,128)(2,1)} fusion(f32[1024,4480]{1,0:T(8,128)} %get-tuple-element.211, bf16[1024,1536]{1,0:T(8,128)(2,1)S(1)} %copy-done.12, bf16[4480,1536]{1,0:T(8,128)(2,1)} %pad_maximum_fusion), kind=kOutput, calls=%fused_computation.54 | convolution fusion | flops 14102036480 | bytes 44433408 | tf_op jit(solution)/shard_map/dot_general | solution.py:24
  604.8 31.6 %fusion.35 = (f32[1024,4480]{1,0:T(8,128)}, bf16[1024,4480]{1,0:T(8,128)(2,1)}) fusion(bf16[1024,1536]{1,0:T(8,128)(2,1)S(1)} %copy-done.15, bf16[1536,4480]{1,0:T(8,128)(2,1)} %pad_maximum_fusion.3), kind=kOutput, calls=%fused_computation.47 | convolution fusion | flops 14180024320 | bytes 44433408 | tf_op jit(solution)/shard_map/dot_general | solution.py:20
  636.4 28.7 %multiply_convert_fusion.4 = bf16[1024,4480]{1,0:T(8,128)(2,1)} fusion(f32[1024,4480]{1,0:T(8,128)} %get-tuple-element.219, bf16[1024,1536]{1,0:T(8,128)(2,1)S(1)} %copy-done.14, bf16[4480,1536]{1,0:T(8,128)(2,1)} %pad_maximum_fusion), kind=kOutput, calls=%fused_computation.52 | convolution fusion | flops 14102036480 | bytes 44433408 | tf_op jit(solution)/shard_map/dot_general | solution.py:24
  811.6 24.3 %token_sum_up.5 = f32[768,2304]{1,0:T(8,128)} custom-call(s32[1]{0:T(128)} %bitcast.1.index_ref, bf16[1024,1536]{1,0:T(8,128)(2,1)} %all-gather.13.cloned.1.call-done.refs_0_, bf16[1024,1536]{1,0:T(8,128)(2,1)} %all-gather.15.cloned.1.call-done.refs_1_, bf16[1024,1536]{1,0:T(8,128)(2,1)} %collective-permute-done.9.refs_2_, ...), custom_call_target="tpu_custom_call" | custom-call | flops 14495514624 | bytes 39321600 | tf_op jit(solution)/shard_map/token_sum_up/pallas_call | solution.py:101
  858.3 22.7 %fusion.55 = f32[1024,1536]{1,0:T(8,128)} fusion(bf16[1024,4480]{1,0:T(8,128)(2,1)} %get-tuple-element.267, bf16[4480,1536]{1,0:T(8,128)(2,1)} %pad_maximum_fusion), kind=kOutput, calls=%fused_computation.129 | convolution fusion | flops 14092861440 | bytes 29229056 | tf_op jit(solution)/shard_map/dot_general | solution.py:20
  881.1 23.2 %token_sum_down.5 = f32[2304,768]{1,0:T(8,128)} custom-call(s32[1]{0:T(128)} %bitcast.3.index_ref, bf16[1024,2304]{1,0:T(8,128)(2,1)} %constant_dynamic-slice_fusion.4.refs_0_, bf16[1024,2304]{1,0:T(8,128)(2,1)} %constant_dynamic-slice_fusion.3.refs_1_, bf16[1024,2304]{1,0:T(8,128)(2,1)} %get-tuple-element.272.refs_2_, ...), custom_call_target="tpu_custom_call" | custom-call | flops 14495514624 | bytes 39321600 | tf_op jit(solution)/shard_map/token_sum_down/pallas_call | solution.py:101
  926.7 28.7 %multiply_convert_fusion.3.refs_4_ = bf16[1024,4480]{1,0:T(8,128)(2,1)} fusion(f32[1024,4480]{1,0:T(8,128)} %get-tuple-element.283, bf16[1024,1536]{1,0:T(8,128)(2,1)S(1)} %copy-done.16, bf16[4480,1536]{1,0:T(8,128)(2,1)} %copy-done.9), kind=kOutput, calls=%fused_computation.51 | convolution fusion | flops 14102036480 | bytes 44433408 | tf_op jit(solution)/shard_map/dot_general | solution.py:24
  979.3 29.7 %multiply_convert_fusion.2.refs_5_ = bf16[1024,4480]{1,0:T(8,128)(2,1)} fusion(f32[1024,4480]{1,0:T(8,128)} %get-tuple-element.288, bf16[1024,1536]{1,0:T(8,128)(2,1)S(1)} %copy-done.17, bf16[4480,1536]{1,0:T(8,128)(2,1)} %copy-done.9), kind=kOutput, calls=%fused_computation.50 | convolution fusion | flops 14102036480 | bytes 44433408 | tf_op jit(solution)/shard_map/dot_general | solution.py:24
  1026.1 36.9 %token_sum_down.6 = f32[4480,768]{1,0:T(8,128)} custom-call(s32[1]{0:T(128)} %bitcast.4.index_ref, bf16[1024,4480]{1,0:T(8,128)(2,1)} %get-tuple-element.303.refs_0_, bf16[1024,4480]{1,0:T(8,128)(2,1)} %get-tuple-element.304.refs_1_, bf16[1024,4480]{1,0:T(8,128)(2,1)} %get-tuple-element.305.refs_2_, bf16[1024,4480]{1,0:T(8,128)(2,1)} %get-tuple-element.306.refs_3_, ...), custom_call_target="tpu_custom_call" | custom-call | flops 28185722880 | bytes 56754176 | tf_op jit(solution)/shard_map/token_sum_down/pallas_call | solution.py:101
  1068.4 23.0 %fusion.58 = f32[1024,1536]{1,0:T(8,128)} fusion(bf16[1024,4480]{1,0:T(8,128)(2,1)} %multiply_convert_fusion.2.refs_5_, bf16[1536,4480]{1,0:T(8,128)(2,1)} %pad_maximum_fusion.1), kind=kOutput, calls=%fused_computation.132 | convolution fusion | flops 14092861440 | bytes 29229056 | tf_op jit(solution)/shard_map/dot_general | solution.py:24
  1091.3 38.1 %token_sum_down.7 = f32[4480,768]{1,0:T(8,128)} custom-call(s32[1]{0:T(128)} %bitcast.5.index_ref, bf16[1024,4480]{1,0:T(8,128)(2,1)} %get-tuple-element.303.refs_0_, bf16[1024,4480]{1,0:T(8,128)(2,1)} %get-tuple-element.304.refs_1_, bf16[1024,4480]{1,0:T(8,128)(2,1)} %get-tuple-element.305.refs_2_, bf16[1024,4480]{1,0:T(8,128)(2,1)} %get-tuple-element.306.refs_3_, ...), custom_call_target="tpu_custom_call" | custom-call | flops 28185722880 | bytes 70516736 | tf_op jit(solution)/shard_map/token_sum_down/pallas_call | solution.py:101
  1181.0 40.8 %token_sum_up.6 = f32[768,4480]{1,0:T(8,128)} custom-call(s32[1]{0:T(128)} %bitcast.6.index_ref, bf16[1024,1536]{1,0:T(8,128)(2,1)} %all-gather.9.cloned.1.call-done.refs_0_, bf16[1024,1536]{1,0:T(8,128)(2,1)} %all-gather.11.cloned.1.call-done.refs_1_, bf16[1024,1536]{1,0:T(8,128)(2,1)} %copy-done.11, bf16[1024,1536]{1,0:T(8,128)(2,1)} %collective-permute-done.7.refs_3_, ...), custom_call_target="tpu_custom_call" | custom-call | flops 28185722880 | bytes 56754176 | tf_op jit(solution)/shard_map/token_sum_up/pallas_call | solution.py:101
  1221.8 82.5 %collective-permute-start.19 = (f32[768,4480]{1,0:T(8,128)}, f32[768,4480]{1,0:T(8,128)}, u32[]{:S(2)}, u32[]{:S(2)}) collective-permute-start(f32[768,4480]{1,0:T(8,128)} %token_sum_up.6), channel_id=1, source_target_pairs={{0,1},{1,0},{2,3},{3,2},{4,5},{5,4},{6,7},{7,6}} | collective-permute-start | bytes 41287688 | tf_op jit(solution)/shard_map/ppermute | solution.py:32
  1341.1 117.8 %collective-permute-done.22 = f32[2304,768]{1,0:T(8,128)} collective-permute-done((f32[2304,768]{1,0:T(8,128)}, f32[2304,768]{1,0:T(8,128)}, u32[]{:S(2)}, u32[]{:S(2)}) %collective-permute-start.22) | collective-permute-done | bytes 7077920 | tf_op jit(solution)/shard_map/ppermute | solution.py:32
  1476.1 42.3 %token_sum_up.7 = f32[768,4480]{1,0:T(8,128)} custom-call(s32[1]{0:T(128)} %bitcast.7.index_ref, bf16[1024,1536]{1,0:T(8,128)(2,1)} %all-gather.9.cloned.1.call-done.refs_0_, bf16[1024,1536]{1,0:T(8,128)(2,1)} %all-gather.11.cloned.1.call-done.refs_1_, bf16[1024,1536]{1,0:T(8,128)(2,1)} %copy-done.11, bf16[1024,1536]{1,0:T(8,128)(2,1)} %collective-permute-done.7.refs_3_, ...), custom_call_target="tpu_custom_call" | custom-call | flops 28185722880 | bytes 70516736 | tf_op jit(solution)/shard_map/token_sum_up/pallas_call | solution.py:101
  (222 shorter events, 551.0 us)
Async XLA Ops:
  12.0 153.2 %collective-permute-start.1 = (bf16[4480,768]{1,0:T(8,128)(2,1)}, bf16[4480,768]{1,0:T(8,128)(2,1)}, u32[]{:S(2)}, u32[]{:S(2)}) collective-permute-start(bf16[4480,768]{1,0:T(8,128)(2,1)} %param.8), channel_id=1, source_target_pairs={{1,2},{2,1},{5,6},{6,5}} | collective-permute-start | bytes 20643848 | tf_op jit(solution)/shard_map/ppermute | solution.py:140
  15.6 394.0 %reduce-scatter.9.cloned.1.call-start = ((), (), s32[]{:S(2)}) async-start(), calls=%async_computation.10 | async-start | bytes 9437184 | tf_op jit(solution)/shard_map/reduce_scatter | solution.py:45
  210.9 249.2 %reduce-scatter.11.cloned.1.call-start = ((), (), s32[]{:S(2)}) async-start(), calls=%async_computation.12 | async-start | bytes 9437184 | tf_op jit(solution)/shard_map/reduce_scatter | solution.py:45
  233.5 230.1 %all-gather.17.cloned.1.call-start = ((), (), s32[]{:S(2)}) async-start(), calls=%async_computation.14 | async-start | bytes 4718592 | tf_op jit(solution)/shard_map/all_gather | solution.py:41
  242.4 260.0 %all-gather.13.cloned.1.call-start = ((), (), s32[]{:S(2)}) async-start(), calls=%async_computation.11 | async-start | bytes 4718592 | tf_op jit(solution)/shard_map/all_gather | solution.py:41
  242.5 170.5 %collective-permute-start.7 = (bf16[1024,1536]{1,0:T(8,128)(2,1)}, bf16[1024,1536]{1,0:T(8,128)(2,1)}, u32[]{:S(2)}, u32[]{:S(2)}) collective-permute-start(bf16[1024,1536]{1,0:T(8,128)(2,1)} %all-gather.11.cloned.1.call-done.refs_1_), channel_id=1, source_target_pairs={{0,4},{4,0},{1,5},{5,1},{2,6},{6,2},{3,7},{7,3}} | collective-permute-start | bytes 9437192 | tf_op jit(solution)/shard_map/ppermute | solution.py:32
  244.0 137.1 %collective-permute-start.3 = (bf16[1024,1536]{1,0:T(8,128)(2,1)}, bf16[1024,1536]{1,0:T(8,128)(2,1)S(1)}, u32[]{:S(2)}, u32[]{:S(2)}) collective-permute-start(bf16[1024,1536]{1,0:T(8,128)(2,1)} %all-gather.9.cloned.1.call-done.refs_0_), channel_id=1, source_target_pairs={{0,4},{4,0},{1,5},{5,1},{2,6},{6,2},{3,7},{7,3}} | collective-permute-start | bytes 9437192 | tf_op jit(solution)/shard_map/ppermute | solution.py:32
  244.5 199.6 %collective-permute-start.6 = (bf16[2240,768]{1,0:T(8,128)(2,1)}, bf16[2240,768]{1,0:T(8,128)(2,1)}, u32[]{:S(2)}, u32[]{:S(2)}) collective-permute-start(bf16[2240,768]{1,0:T(8,128)(2,1)} %collective-permute-done.5), channel_id=1, source_target_pairs={{1,5},{5,1},{2,6},{6,2}} | collective-permute-start | bytes 10321928 | tf_op jit(solution)/shard_map/ppermute | solution.py:144
  463.5 139.6 %all-gather.19.cloned.1.call-start = ((), (), s32[]{:S(2)}) async-start(), calls=%async_computation.15 | async-start | bytes 4718592 | tf_op jit(solution)/shard_map/all_gather | solution.py:41
  463.6 285.5 %collective-permute-start.11 = (bf16[1024,1536]{1,0:T(8,128)(2,1)}, bf16[1024,1536]{1,0:T(8,128)(2,1)}, u32[]{:S(2)}, u32[]{:S(2)}) collective-permute-start(bf16[1024,1536]{1,0:T(8,128)(2,1)} %all-gather.17.cloned.1.call-done.refs_4_), channel_id=1, source_target_pairs={{0,4},{4,0},{1,5},{5,1},{2,6},{6,2},{3,7},{7,3}} | collective-permute-start | bytes 9437192 | tf_op jit(solution)/shard_map/ppermute | solution.py:32
  465.1 280.5 %reduce-scatter.13.cloned.1.call-start = ((), (), s32[]{:S(2)}) async-start(), calls=%async_computation.16 | async-start | bytes 9437184 | tf_op jit(solution)/shard_map/reduce_scatter | solution.py:45
  502.5 191.0 %collective-permute-start.9 = (bf16[1024,1536]{1,0:T(8,128)(2,1)}, bf16[1024,1536]{1,0:T(8,128)(2,1)}, u32[]{:S(2)}, u32[]{:S(2)}) collective-permute-start(bf16[1024,1536]{1,0:T(8,128)(2,1)} %all-gather.13.cloned.1.call-done.refs_0_), channel_id=1, source_target_pairs={{0,4},{4,0},{1,5},{5,1},{2,6},{6,2},{3,7},{7,3}} | collective-permute-start | bytes 9437192 | tf_op jit(solution)/shard_map/ppermute | solution.py:32
  581.1 148.2 %collective-permute-start.10 = (bf16[1024,1536]{1,0:T(8,128)(2,1)}, bf16[1024,1536]{1,0:T(8,128)(2,1)}, u32[]{:S(2)}, u32[]{:S(2)}) collective-permute-start(bf16[1024,1536]{1,0:T(8,128)(2,1)} %all-gather.15.cloned.1.call-done.refs_1_), channel_id=1, source_target_pairs={{0,4},{4,0},{1,5},{5,1},{2,6},{6,2},{3,7},{7,3}} | collective-permute-start | bytes 9437192 | tf_op jit(solution)/shard_map/ppermute | solution.py:32
  603.1 205.1 %reduce-scatter.15.cloned.1.call-start = ((), (), s32[]{:S(2)}) async-start(), calls=%async_computation.17 | async-start | bytes 9437184 | tf_op jit(solution)/shard_map/reduce_scatter | solution.py:45
  603.2 160.3 %collective-permute-start.12 = (bf16[1024,1536]{1,0:T(8,128)(2,1)}, bf16[1024,1536]{1,0:T(8,128)(2,1)}, u32[]{:S(2)}, u32[]{:S(2)}) collective-permute-start(bf16[1024,1536]{1,0:T(8,128)(2,1)} %all-gather.19.cloned.1.call-done.refs_5_), channel_id=1, source_target_pairs={{0,4},{4,0},{1,5},{5,1},{2,6},{6,2},{3,7},{7,3}} | collective-permute-start | bytes 9437192 | tf_op jit(solution)/shard_map/ppermute | solution.py:32
  704.7 176.3 %all-gather.21.cloned.1.call-start = ((), (), s32[]{:S(2)}) async-start(), calls=%async_computation.19 | async-start | bytes 4718592 | tf_op jit(solution)/shard_map/all_gather | solution.py:41
  858.2 471.9 %reduce-scatter.17.cloned.1.call-start = ((), (), s32[]{:S(2)}) async-start(), calls=%async_computation.18 | async-start | bytes 9437184 | tf_op jit(solution)/shard_map/reduce_scatter | solution.py:45
  881.0 452.7 %reduce-scatter.19.cloned.1.call-start = ((), (), s32[]{:S(2)}) async-start(), calls=%async_computation.21 | async-start | bytes 9437184 | tf_op jit(solution)/shard_map/reduce_scatter | solution.py:45
  955.4 381.6 %reduce-scatter.21.cloned.1.call-start = ((), (), s32[]{:S(2)}) async-start(), calls=%async_computation.22 | async-start | bytes 9437184 | tf_op jit(solution)/shard_map/reduce_scatter | solution.py:45
  1066.6 451.8 %reduce-scatter.23.cloned.1.call-start = ((), (), s32[]{:S(2)}) async-start(), calls=%async_computation.23 | async-start | bytes 9437184 | tf_op jit(solution)/shard_map/reduce_scatter | solution.py:45
  1066.6 244.9 %collective-permute-start.21 = (f32[768,2304]{1,0:T(8,128)}, f32[768,2304]{1,0:T(8,128)}, u32[]{:S(2)}, u32[]{:S(2)}) collective-permute-start(f32[768,2304]{1,0:T(8,128)} %token_sum_up.5), channel_id=1, source_target_pairs={{0,4},{4,0},{1,5},{5,1},{2,6},{6,2},{3,7},{7,3}} | collective-permute-start | bytes 21233672 | tf_op jit(solution)/shard_map/ppermute | solution.py:32
  1221.8 254.3 %collective-permute-start.19 = (f32[768,4480]{1,0:T(8,128)}, f32[768,4480]{1,0:T(8,128)}, u32[]{:S(2)}, u32[]{:S(2)}) collective-permute-start(f32[768,4480]{1,0:T(8,128)} %token_sum_up.6), channel_id=1, source_target_pairs={{0,1},{1,0},{2,3},{3,2},{4,5},{5,4},{6,7},{7,6}} | collective-permute-start | bytes 41287688 | tf_op jit(solution)/shard_map/ppermute | solution.py:32
  1304.2 154.6 %collective-permute-start.22 = (f32[2304,768]{1,0:T(8,128)}, f32[2304,768]{1,0:T(8,128)}, u32[]{:S(2)}, u32[]{:S(2)}) collective-permute-start(f32[2304,768]{1,0:T(8,128)} %broadcast_select_fusion.12), channel_id=1, source_target_pairs={{0,4},{4,0},{1,5},{5,1},{2,6},{6,2},{3,7},{7,3}} | collective-permute-start | bytes 21233672 | tf_op jit(solution)/shard_map/ppermute | solution.py:32
  1305.9 219.1 %collective-permute-start.20 = (f32[4480,768]{1,0:T(8,128)}, f32[4480,768]{1,0:T(8,128)}, u32[]{:S(2)}, u32[]{:S(2)}) collective-permute-start(f32[4480,768]{1,0:T(8,128)} %token_sum_down.7), channel_id=1, source_target_pairs={{1,2},{2,1},{5,6},{6,5}} | collective-permute-start | bytes 41287688 | tf_op jit(solution)/shard_map/ppermute | solution.py:140
  (53 other events, 2250.0 us)
Sparse Core Ops, SparseCore 0:
  12.1 61.2 all-gather.8
  74.8 59.0 all-gather.10
  211.0 95.4 reduce-scatter.8
  308.7 80.9 reduce-scatter.10
  391.0 42.1 all-gather.16
  460.2 42.2 all-gather.12
  504.5 42.1 all-gather.14
  548.2 42.1 all-gather.18
  603.2 74.4 reduce-scatter.12
  704.8 72.9 reduce-scatter.14
  808.2 41.0 all-gather.20
  858.3 40.9 all-gather.22
  901.6 74.3 reduce-scatter.16
  978.1 74.3 reduce-scatter.18
  1066.7 108.4 reduce-scatter.20
  1311.7 107.0 reduce-scatter.22

commit v4 on v3

--- a/solution.py
+++ b/solution.py
@@ -58,6 +58,15 @@
 
 def grad_pre_of(slope, grad, down):
     return (dot_last(grad, down) * slope).astype(jnp.bfloat16)
+
+
+def hidden_and_pre(acts, up):
+    pre = dot(acts, up)
+    return pre, gelu_tanh(pre).astype(jnp.bfloat16)
+
+
+def grad_pre_from(pre, grad, down):
+    return gelu_grad(pre, dot_last(grad, down)).astype(jnp.bfloat16)
 
 
 def add_round(base, total):
@@ -166,20 +175,21 @@
         g0, g1 = split(grad_out)
 
         up1_other = swap(w_up1, "row")
-        moved1 = hop(w_down1)
+        half1 = hop(half_of(w_down1, dep, 0))
         xa0 = gather_cols(x0)
         xa1 = gather_cols(x1)
         up2_other = swap(after(w_up2, up1_other), "row")
         up1 = run(lambda a, b: in_order(row, a, b, 0), w_up1, up1_other)
 
         pre1_0, hid1_0 = run(hidden_of, xa0, up1)
-        ga0 = gather_cols(after(g0, xa1))
+        ga0 = gather_cols(after(g0, xa0))
         xf0 = swap(xa0, "dep")
+        half1_far = hop_far(half1)
         pre1_1, hid1_1 = run(hidden_of, xa1, up1)
         xf1 = swap(xa1, "dep")
-        tile1 = run(own_or, w_down1, moved1)
+        tile1 = run(own_or_halves, w_down1, half1, half1_far)
         tile1_other = swap(tile1, "row")
-        half2 = hop(half_of(after(w_down2, moved1), dep, 0))
+        half2 = hop(half_of(after(w_down2, half1_far), dep, 0))
         down1 = run(lambda a, b: in_order(row, a, b, 1), tile1, tile1_other)
         part0 = run(dot, hid1_0, down1)
         zs0 = scatter_cols(part0)
@@ -199,27 +209,30 @@
         ga1 = gather_cols(after(g1, z1))
         down2 = run(lambda a, b: in_order(row, a, b, 1), tile2, tile2_other)
 
+        up2_win = run(lambda a: win(a, 1), up2)
+        down2_win = run(lambda a: win(a, 0), down2)
+        za0 = after(za0, down2_win)
+
         zf0 = swap(za0, "dep")
-        pre2, hid2_0 = run(hidden_of, za0, up2)
-        gpre2_0 = run(grad_pre_of, pre2, ga0, down2)
+        pre2, hid2_0 = run(hidden_and_pre, za0, up2)
+        gpre2_0 = run(grad_pre_from, pre2, ga0, down2)
         zf1 = swap(after(za1, gpre2_0), "dep")
         part0 = run(dot_last, gpre2_0, up2)
         ds0 = scatter_cols(part0)
         gf1 = swap(after(ga1, part0), "dep")
-        pre2, hid2_1 = run(hidden_of, za1, up2)
-        gpre2_1 = run(grad_pre_of, pre2, ga1, down2)
-        ds1 = scatter_cols(run(dot_last, gpre2_1, up2))
-
-        up2_win = run(lambda a: win(a, 1), up2)
+        pre2, hid2_1 = run(hidden_and_pre, za1, up2)
+        gpre2_1 = run(grad_pre_from, pre2, ga1, down2)
+        part1 = run(dot_last, gpre2_1, up2)
+        ds1 = scatter_cols(part1)
+
         pre2_f0, hid2_f0 = run(hidden_of, zf0, up2_win)
         pre2_f1, hid2_f1 = run(hidden_of, zf1, up2_win)
         dz0 = run(add_round, g0, ds0)
         dza0 = gather_cols(dz0)
-        down2_win = win(down2, 0)
         gpre2_f0 = run(grad_pre_of, pre2_f0, gf0, down2_win)
         gpre2_f1 = run(grad_pre_of, pre2_f1, gf1, down2_win)
         acts2 = (za0, za1), (zf0, zf1)
-        gpres2 = (win(gpre2_0, 1), win(gpre2_1, 1)), (gpre2_f0, gpre2_f1)
+        gpres2 = (win(after(gpre2_0, part1), 1), win(after(gpre2_1, part1), 1)), (gpre2_f0, gpre2_f1)
         sent = run(up_term, acts2, gpres2, 1 - row)
         got = swap(sent, "row")
         dz1 = run(add_round, g1, ds1)
@@ -245,22 +258,23 @@
         sent = run(down_term, hids1, grads1, 1 - row)
         got = swap(sent, "row")
         xs1 = scatter_cols(run(dot_last, gpre1_1, up1))
-        down_a = run(down_term, hids1, grads1, row, got)
-        down_a_moved = hop(down_a)
         down_b = run(own_or, down_b, down_b_moved)
         grad_down2 = join(down_b, 0)
+        down_a = run(down_term, hids1, grads1, row, got)
+        half_a = hop(half_of(down_a, dep, 0))
         gpre1_f0 = run(grad_pre_of, hid1_f0[0], dzf0, down1)
         gpre1_f1 = run(grad_pre_of, hid1_f1[0], dzf1, down1)
         acts1 = (xa0, xa1), (xf0, xf1)
         gpres1 = (gpre1_0, gpre1_1), (gpre1_f0, gpre1_f1)
         sent = run(up_term, acts1, gpres1, 1 - row)
         got = swap(sent, "row")
+        half_a_far = hop_far(after(half_a, sent))
         y0 = run(add_round, z0, ys0)
         y1 = run(add_round, z1, ys1)
         dx0 = run(add_round, dz0, xs0)
         grad_up1 = run(up_term, acts1, gpres1, row, got)
         dx1 = run(add_round, dz1, xs1)
-        grad_down1 = own_or(down_a, down_a_moved)
+        grad_down1 = own_or_halves(down_a, half_a, half_a_far)
         y_out = jnp.concatenate([y0, y1], axis=0)
         grad_x = jnp.concatenate([dx0, dx1], axis=0)
         return y_out, grad_x, grad_up1, grad_down1, grad_up2, grad_down2

time: 1550 us -> 1610 us (1.039)
  starting transfers between devices: 114 us -> 168 us
    ppermute x18, starting transfers between devices: 96.1 us -> 149 us  [swap(): return lax.ppermute(value, axis, [(0, 1), (1, 0)])]
    all_gather x8, waiting for transfers between devices: 109 us -> 73.2 us  [gather_cols(): return lax.all_gather(value, 'col', axis=1, tiled=True)]
    ppermute x18, waiting for transfers between devices: 270 us -> 301 us  [swap(): return lax.ppermute(value, axis, [(0, 1), (1, 0)])]
    select_n x5 -> x7, other arithmetic: 32.2 us -> 46 us  [in_order(): low = jnp.where(index == 0, mine, other)]
  transfers between devices with their start and end apart: 39 -> 41, of which waited for: 8 -> 10; matrix products, arithmetic and copies ran while one was open for 47% -> 45% of each run, Pallas kernels for 16% -> 16%
where the time goes in v4:
time: 1610 us; the launch traced here: 1600 us
  matrix products  568 us (35%)
  waiting for transfers between devices  375 us (23%)
  Pallas kernels  250 us (16%)
  starting transfers between devices  168 us (10%)
  other arithmetic  167 us (10%)
  local copies, waits for them, and re-layouts  59.5 us (4%)
    ppermute x18, waiting for transfers between devices, swap(): return lax.ppermute(value, axis, [(0, 1), (1, 0)])  301 us
    dot_general x12, matrix products, dot(): return jnp.dot(left_op, right_op, preferred_element_type=jnp.float32)  289 us
    dot_general x12, matrix products, dot_last(): lax.dot_general(left_op, right_op, (((1,), (1,)), ((), ())), preferred_el...  280 us
    pallas_call x8, Pallas kernels, token_sum(): pl.pallas_call(token_sum_kernel, out_shape=jax.ShapeDtypeStruct(shape, jn...  250 us
    ppermute x18, starting transfers between devices, swap(): return lax.ppermute(value, axis, [(0, 1), (1, 0)])  149 us
    all_gather x8, waiting for transfers between devices, gather_cols(): return lax.all_gather(value, 'col', axis=1, tiled=True)  73.2 us
    select_n x7, other arithmetic, in_order(): low = jnp.where(index == 0, mine, other)  46 us
    select_n x4, other arithmetic, own_or(): return jnp.where(col == row, shard, moved)  40.2 us
  transfers between devices with their start and end apart: 41, of which 10 were waited for; matrix products, arithmetic and copies ran while one was open for 45% of the time, Pallas kernels for 16%

profile of v4, /device:TPU:0, one launch (start us, length us, event | category | flops | bytes accessed | tf_op | source)
XLA Modules:
  0.0 1603.7 jit_solution(11770259469227916443)
XLA Ops:
  32.4 47.2 %all-gather.9.cloned.1.call-done.refs_0_ = bf16[1024,1536]{1,0:T(8,128)(2,1)} async-done(((bf16[1024,768]{1,0:T(8,128)(2,1)}), bf16[1024,1536]{1,0:T(8,128)(2,1)}) %all-gather.9.cloned.1.call-update) | async-done | bytes 3145744 | tf_op jit(solution)/shard_map/all_gather | solution.py:41
  79.6 31.1 %fusion.5 = (f32[1024,4480]{1,0:T(8,128)}, bf16[1024,4480]{1,0:T(8,128)(2,1)}) fusion(bf16[1024,1536]{1,0:T(8,128)(2,1)} %all-gather.9.cloned.1.call-done.refs_0_, bf16[1536,4480]{1,0:T(8,128)(2,1)} %pad_maximum_fusion), kind=kOutput, calls=%fused_computation.19 | convolution fusion | flops 14180024320 | bytes 44433408 | tf_op jit(solution)/shard_map/dot_general | solution.py:20
  123.2 31.4 %fusion.11 = (f32[1024,4480]{1,0:T(8,128)}, bf16[1024,4480]{1,0:T(8,128)(2,1)}) fusion(bf16[1024,1536]{1,0:T(8,128)(2,1)} %all-gather.11.cloned.1.call-done.refs_1_, bf16[1536,4480]{1,0:T(8,128)(2,1)} %pad_maximum_fusion), kind=kOutput, calls=%fused_computation.25 | convolution fusion | flops 14180024320 | bytes 44433408 | tf_op jit(solution)/shard_map/dot_general | solution.py:20
  265.9 52.1 %collective-permute-done.4.refs_2_ = bf16[1024,1536]{1,0:T(8,128)(2,1)S(1)} collective-permute-done((bf16[1024,1536]{1,0:T(8,128)(2,1)}, bf16[1024,1536]{1,0:T(8,128)(2,1)S(1)}, u32[]{:S(2)}, u32[]{:S(2)}) %collective-permute-start.4) | collective-permute-done | bytes 3145760 | tf_op jit(solution)/shard_map/ppermute | solution.py:32
  319.7 26.9 %fusion.17 = (f32[1024,4480]{1,0:T(8,128)}, bf16[1024,4480]{1,0:T(8,128)(2,1)}) fusion(bf16[1024,1536]{1,0:T(8,128)(2,1)S(1)} %collective-permute-done.4.refs_2_, bf16[1536,4480]{1,0:T(8,128)(2,1)S(1)} %bitcast.59), kind=kOutput, calls=%fused_computation.31 | convolution fusion | flops 14180024320 | bytes 44433408 | tf_op jit(solution)/shard_map/dot_general | solution.py:20
  350.0 35.5 %collective-permute-done.8.refs_3_ = bf16[1024,1536]{1,0:T(8,128)(2,1)} collective-permute-done((bf16[1024,1536]{1,0:T(8,128)(2,1)}, bf16[1024,1536]{1,0:T(8,128)(2,1)}, u32[]{:S(2)}, u32[]{:S(2)}) %collective-permute-start.8) | collective-permute-done | bytes 3145760 | tf_op jit(solution)/shard_map/ppermute | solution.py:32
  385.5 31.3 %fusion.23 = (f32[1024,4480]{1,0:T(8,128)}, bf16[1024,4480]{1,0:T(8,128)(2,1)}) fusion(bf16[1024,1536]{1,0:T(8,128)(2,1)} %collective-permute-done.8.refs_3_, bf16[1536,4480]{1,0:T(8,128)(2,1)} %pad_maximum_fusion), kind=kOutput, calls=%fused_computation.37 | convolution fusion | flops 14180024320 | bytes 44433408 | tf_op jit(solution)/shard_map/dot_general | solution.py:20
  485.0 24.4 %fusion.45 = (bf16[1024,4480]{1,0:T(8,128)(2,1)}, f32[1024,4480]{1,0:T(8,128)}) fusion(bf16[1024,1536]{1,0:T(8,128)(2,1)} %all-gather.13.cloned.1.call-done.refs_0_, bf16[1536,4480]{1,0:T(8,128)(2,1)} %pad_maximum_fusion.2), kind=kOutput, calls=%fused_computation.59 | convolution fusion | flops 14134149120 | bytes 44433408 | tf_op jit(solution)/shard_map/dot_general | solution.py:20
  509.3 30.2 %fusion.30 = bf16[1024,4480]{1,0:T(8,128)(2,1)} fusion(f32[1024,4480]{1,0:T(8,128)} %get-tuple-element.221, bf16[1024,1536]{1,0:T(8,128)(2,1)S(1)} %copy-done.11, bf16[4480,1536]{1,0:T(8,128)(2,1)} %copy-done), kind=kOutput, calls=%fused_computation.44 | convolution fusion | flops 14184611840 | bytes 44433408 | tf_op jit(solution)/shard_map/dot_general | solution.py:24
  561.7 24.5 %fusion.53 = (bf16[1024,4480]{1,0:T(8,128)(2,1)}, f32[1024,4480]{1,0:T(8,128)}) fusion(bf16[1024,1536]{1,0:T(8,128)(2,1)} %all-gather.15.cloned.1.call-done.refs_1_, bf16[1536,4480]{1,0:T(8,128)(2,1)} %pad_maximum_fusion.2), kind=kOutput, calls=%fused_computation.67 | convolution fusion | flops 14134149120 | bytes 44433408 | tf_op jit(solution)/shard_map/dot_general | solution.py:20
  586.1 31.6 %fusion.37 = bf16[1024,4480]{1,0:T(8,128)(2,1)} fusion(f32[1024,4480]{1,0:T(8,128)} %get-tuple-element.229, bf16[1024,1536]{1,0:T(8,128)(2,1)} %all-gather.19.cloned.1.call-done.refs_5_, bf16[4480,1536]{1,0:T(8,128)(2,1)} %copy-done), kind=kOutput, calls=%fused_computation.51 | convolution fusion | flops 14184611840 | bytes 44433408 | tf_op jit(solution)/shard_map/dot_general | solution.py:24
  668.9 41.8 %collective-permute-done.11.refs_3_ = bf16[1024,1536]{1,0:T(8,128)(2,1)} collective-permute-done((bf16[1024,1536]{1,0:T(8,128)(2,1)S(1)}, bf16[1024,1536]{1,0:T(8,128)(2,1)}, u32[]{:S(2)}, u32[]{:S(2)}) %collective-permute-start.11) | collective-permute-done | bytes 3145760 | tf_op jit(solution)/shard_map/ppermute | solution.py:32
  744.7 31.8 %collective-permute-done.13.refs_7_ = bf16[1024,1536]{1,0:T(8,128)(2,1)} collective-permute-done((bf16[1024,1536]{1,0:T(8,128)(2,1)}, bf16[1024,1536]{1,0:T(8,128)(2,1)}, u32[]{:S(2)}, u32[]{:S(2)}) %collective-permute-start.13) | collective-permute-done | bytes 3145760 | tf_op jit(solution)/shard_map/ppermute | solution.py:32
  824.4 24.5 %token_sum_up.5 = f32[768,2304]{1,0:T(8,128)} custom-call(s32[1]{0:T(128)} %bitcast.1.index_ref, bf16[1024,1536]{1,0:T(8,128)(2,1)} %all-gather.13.cloned.1.call-done.refs_0_, bf16[1024,1536]{1,0:T(8,128)(2,1)} %all-gather.15.cloned.1.call-done.refs_1_, bf16[1024,1536]{1,0:T(8,128)(2,1)} %collective-permute-done.10.refs_2_, ...), custom_call_target="tpu_custom_call" | custom-call | flops 14495514624 | bytes 39321600 | tf_op jit(solution)/shard_map/token_sum_up/pallas_call | solution.py:110
  872.2 22.6 %fusion.72 = f32[1024,1536]{1,0:T(8,128)} fusion(bf16[1024,4480]{1,0:T(8,128)(2,1)} %get-tuple-element.278, bf16[4480,1536]{1,0:T(8,128)(2,1)} %copy-done), kind=kOutput, calls=%fused_computation.149 | convolution fusion | flops 14092861440 | bytes 29229056 | tf_op jit(solution)/shard_map/dot_general | solution.py:20
  894.9 23.2 %token_sum_down.5 = f32[2304,768]{1,0:T(8,128)} custom-call(s32[1]{0:T(128)} %bitcast.3.index_ref, bf16[1024,2304]{1,0:T(8,128)(2,1)} %constant_dynamic-slice_fusion.4.refs_0_, bf16[1024,2304]{1,0:T(8,128)(2,1)} %constant_dynamic-slice_fusion.3.refs_1_, bf16[1024,2304]{1,0:T(8,128)(2,1)} %get-tuple-element.283.refs_2_, ...), custom_call_target="tpu_custom_call" | custom-call | flops 14495514624 | bytes 39321600 | tf_op jit(solution)/shard_map/token_sum_down/pallas_call | solution.py:110
  941.3 28.7 %multiply_convert_fusion.3.refs_4_ = bf16[1024,4480]{1,0:T(8,128)(2,1)} fusion(f32[1024,4480]{1,0:T(8,128)} %get-tuple-element.294, bf16[1024,1536]{1,0:T(8,128)(2,1)S(1)} %copy-done.13, bf16[4480,1536]{1,0:T(8,128)(2,1)} %copy-done.7), kind=kOutput, calls=%fused_computation.71 | convolution fusion | flops 14102036480 | bytes 44433408 | tf_op jit(solution)/shard_map/dot_general | solution.py:24
  991.9 29.9 %multiply_convert_fusion.2.refs_5_ = bf16[1024,4480]{1,0:T(8,128)(2,1)} fusion(f32[1024,4480]{1,0:T(8,128)} %get-tuple-element.299, bf16[1024,1536]{1,0:T(8,128)(2,1)S(1)} %copy-done.14, bf16[4480,1536]{1,0:T(8,128)(2,1)} %copy-done.7), kind=kOutput, calls=%fused_computation.70 | convolution fusion | flops 14102036480 | bytes 44433408 | tf_op jit(solution)/shard_map/dot_general | solution.py:24
  1021.8 37.2 %token_sum_down.6 = f32[4480,768]{1,0:T(8,128)} custom-call(s32[1]{0:T(128)} %bitcast.4.index_ref, bf16[1024,4480]{1,0:T(8,128)(2,1)} %get-tuple-element.316.refs_0_, bf16[1024,4480]{1,0:T(8,128)(2,1)} %get-tuple-element.317.refs_1_, bf16[1024,4480]{1,0:T(8,128)(2,1)} %get-tuple-element.318.refs_2_, bf16[1024,4480]{1,0:T(8,128)(2,1)} %get-tuple-element.319.refs_3_, ...), custom_call_target="tpu_custom_call" | custom-call | flops 28185722880 | bytes 56754176 | tf_op jit(solution)/shard_map/token_sum_down/pallas_call | solution.py:110
  1093.2 38.6 %token_sum_down.7 = f32[4480,768]{1,0:T(8,128)} custom-call(s32[1]{0:T(128)} %bitcast.5.index_ref, bf16[1024,4480]{1,0:T(8,128)(2,1)} %get-tuple-element.316.refs_0_, bf16[1024,4480]{1,0:T(8,128)(2,1)} %get-tuple-element.317.refs_1_, bf16[1024,4480]{1,0:T(8,128)(2,1)} %get-tuple-element.318.refs_2_, bf16[1024,4480]{1,0:T(8,128)(2,1)} %get-tuple-element.319.refs_3_, ...), custom_call_target="tpu_custom_call" | custom-call | flops 28185722880 | bytes 70516736 | tf_op jit(solution)/shard_map/token_sum_down/pallas_call | solution.py:110
  1176.2 40.8 %token_sum_up.6 = f32[768,4480]{1,0:T(8,128)} custom-call(s32[1]{0:T(128)} %bitcast.6.index_ref, bf16[1024,1536]{1,0:T(8,128)(2,1)} %all-gather.9.cloned.1.call-done.refs_0_, bf16[1024,1536]{1,0:T(8,128)(2,1)} %all-gather.11.cloned.1.call-done.refs_1_, bf16[1024,1536]{1,0:T(8,128)(2,1)} %copy-done.10, bf16[1024,1536]{1,0:T(8,128)(2,1)} %collective-permute-done.8.refs_3_, ...), custom_call_target="tpu_custom_call" | custom-call | flops 28185722880 | bytes 56754176 | tf_op jit(solution)/shard_map/token_sum_up/pallas_call | solution.py:110
  1217.0 121.8 %collective-permute-start.20 = (f32[768,4480]{1,0:T(8,128)}, f32[768,4480]{1,0:T(8,128)}, u32[]{:S(2)}, u32[]{:S(2)}) collective-permute-start(f32[768,4480]{1,0:T(8,128)} %token_sum_up.6), channel_id=1, source_target_pairs={{0,1},{1,0},{2,3},{3,2},{4,5},{5,4},{6,7},{7,6}} | collective-permute-start | bytes 41287688 | tf_op jit(solution)/shard_map/ppermute | solution.py:32
  1371.1 122.3 %collective-permute-done.24 = f32[2304,768]{1,0:T(8,128)} collective-permute-done((f32[2304,768]{1,0:T(8,128)}, f32[2304,768]{1,0:T(8,128)}, u32[]{:S(2)}, u32[]{:S(2)}) %collective-permute-start.24) | collective-permute-done | bytes 7077920 | tf_op jit(solution)/shard_map/ppermute | solution.py:32
  1524.6 42.3 %token_sum_up.7 = f32[768,4480]{1,0:T(8,128)} custom-call(s32[1]{0:T(128)} %bitcast.7.index_ref, bf16[1024,1536]{1,0:T(8,128)(2,1)} %all-gather.9.cloned.1.call-done.refs_0_, bf16[1024,1536]{1,0:T(8,128)(2,1)} %all-gather.11.cloned.1.call-done.refs_1_, bf16[1024,1536]{1,0:T(8,128)(2,1)} %copy-done.10, bf16[1024,1536]{1,0:T(8,128)(2,1)} %collective-permute-done.8.refs_3_, ...), custom_call_target="tpu_custom_call" | custom-call | flops 28185722880 | bytes 70516736 | tf_op jit(solution)/shard_map/token_sum_up/pallas_call | solution.py:110
  (210 shorter events, 617.6 us)
Async XLA Ops:
  17.4 329.2 %reduce-scatter.9.cloned.1.call-start = ((), (), s32[]{:S(2)}) async-start(), calls=%async_computation.10 | async-start | bytes 9437184 | tf_op jit(solution)/shard_map/reduce_scatter | solution.py:45
  17.5 137.1 %collective-permute-start.2 = (bf16[2240,768]{1,0:T(8,128)(2,1)S(1)}, bf16[2240,768]{1,0:T(8,128)(2,1)}, u32[]{:S(2)}, u32[]{:S(2)}) collective-permute-start(bf16[2240,768]{1,0:T(8,128)(2,1)S(1)} %collective-permute-done.1), channel_id=1, source_target_pairs={{1,5},{5,1},{2,6},{6,2}} | collective-permute-start | bytes 10321928 | tf_op jit(solution)/shard_map/ppermute | solution.py:153
  216.6 220.8 %reduce-scatter.11.cloned.1.call-start = ((), (), s32[]{:S(2)}) async-start(), calls=%async_computation.12 | async-start | bytes 9437184 | tf_op jit(solution)/shard_map/reduce_scatter | solution.py:45
  238.8 202.1 %all-gather.17.cloned.1.call-start = ((), (), s32[]{:S(2)}) async-start(), calls=%async_computation.14 | async-start | bytes 4718592 | tf_op jit(solution)/shard_map/all_gather | solution.py:41
  247.7 235.8 %all-gather.13.cloned.1.call-start = ((), (), s32[]{:S(2)}) async-start(), calls=%async_computation.11 | async-start | bytes 4718592 | tf_op jit(solution)/shard_map/all_gather | solution.py:41
  247.8 137.7 %collective-permute-start.8 = (bf16[1024,1536]{1,0:T(8,128)(2,1)}, bf16[1024,1536]{1,0:T(8,128)(2,1)}, u32[]{:S(2)}, u32[]{:S(2)}) collective-permute-start(bf16[1024,1536]{1,0:T(8,128)(2,1)} %all-gather.11.cloned.1.call-done.refs_1_), channel_id=1, source_target_pairs={{0,4},{4,0},{1,5},{5,1},{2,6},{6,2},{3,7},{7,3}} | collective-permute-start | bytes 9437192 | tf_op jit(solution)/shard_map/ppermute | solution.py:32
  249.8 167.0 %collective-permute-start.7 = (bf16[2240,768]{1,0:T(8,128)(2,1)}, bf16[2240,768]{1,0:T(8,128)(2,1)}, u32[]{:S(2)}, u32[]{:S(2)}) collective-permute-start(bf16[2240,768]{1,0:T(8,128)(2,1)} %collective-permute-done.6), channel_id=1, source_target_pairs={{1,5},{5,1},{2,6},{6,2}} | collective-permute-start | bytes 10321928 | tf_op jit(solution)/shard_map/ppermute | solution.py:153
  437.3 124.2 %all-gather.15.cloned.1.call-start = ((), (), s32[]{:S(2)}) async-start(), calls=%async_computation.13 | async-start | bytes 4718592 | tf_op jit(solution)/shard_map/all_gather | solution.py:41
  440.8 145.3 %all-gather.19.cloned.1.call-start = ((), (), s32[]{:S(2)}) async-start(), calls=%async_computation.15 | async-start | bytes 4718592 | tf_op jit(solution)/shard_map/all_gather | solution.py:41
  440.9 289.7 %collective-permute-start.12 = (bf16[1024,1536]{1,0:T(8,128)(2,1)}, bf16[1024,1536]{1,0:T(8,128)(2,1)}, u32[]{:S(2)}, u32[]{:S(2)}) collective-permute-start(bf16[1024,1536]{1,0:T(8,128)(2,1)} %all-gather.17.cloned.1.call-done.refs_4_), channel_id=1, source_target_pairs={{0,4},{4,0},{1,5},{5,1},{2,6},{6,2},{3,7},{7,3}} | collective-permute-start | bytes 9437192 | tf_op jit(solution)/shard_map/ppermute | solution.py:32
  441.6 285.5 %reduce-scatter.13.cloned.1.call-start = ((), (), s32[]{:S(2)}) async-start(), calls=%async_computation.16 | async-start | bytes 9437184 | tf_op jit(solution)/shard_map/reduce_scatter | solution.py:45
  483.5 166.4 %collective-permute-start.10 = (bf16[1024,1536]{1,0:T(8,128)(2,1)}, bf16[1024,1536]{1,0:T(8,128)(2,1)}, u32[]{:S(2)}, u32[]{:S(2)}) collective-permute-start(bf16[1024,1536]{1,0:T(8,128)(2,1)} %all-gather.13.cloned.1.call-done.refs_0_), channel_id=1, source_target_pairs={{0,4},{4,0},{1,5},{5,1},{2,6},{6,2},{3,7},{7,3}} | collective-permute-start | bytes 9437192 | tf_op jit(solution)/shard_map/ppermute | solution.py:32
  561.6 259.4 %reduce-scatter.15.cloned.1.call-start = ((), (), s32[]{:S(2)}) async-start(), calls=%async_computation.17 | async-start | bytes 9437184 | tf_op jit(solution)/shard_map/reduce_scatter | solution.py:45
  640.1 136.4 %collective-permute-start.13 = (bf16[1024,1536]{1,0:T(8,128)(2,1)}, bf16[1024,1536]{1,0:T(8,128)(2,1)}, u32[]{:S(2)}, u32[]{:S(2)}) collective-permute-start(bf16[1024,1536]{1,0:T(8,128)(2,1)} %all-gather.19.cloned.1.call-done.refs_5_), channel_id=1, source_target_pairs={{0,4},{4,0},{1,5},{5,1},{2,6},{6,2},{3,7},{7,3}} | collective-permute-start | bytes 9437192 | tf_op jit(solution)/shard_map/ppermute | solution.py:32
  641.6 229.7 %all-gather.21.cloned.1.call-start = ((), (), s32[]{:S(2)}) async-start(), calls=%async_computation.19 | async-start | bytes 4718592 | tf_op jit(solution)/shard_map/all_gather | solution.py:41
  871.3 641.1 %reduce-scatter.17.cloned.1.call-start = ((), (), s32[]{:S(2)}) async-start(), calls=%async_computation.18 | async-start | bytes 9437184 | tf_op jit(solution)/shard_map/reduce_scatter | solution.py:45
  871.3 150.5 %collective-permute-start.16 = (bf16[1024,1536]{1,0:T(8,128)(2,1)}, bf16[1024,1536]{1,0:T(8,128)(2,1)}, u32[]{:S(2)}, u32[]{:S(2)}) collective-permute-start(bf16[1024,1536]{1,0:T(8,128)(2,1)} %all-gather.21.cloned.1.call-done.refs_4_), channel_id=1, source_target_pairs={{0,4},{4,0},{1,5},{5,1},{2,6},{6,2},{3,7},{7,3}} | collective-permute-start | bytes 9437192 | tf_op jit(solution)/shard_map/ppermute | solution.py:32
  894.8 620.4 %reduce-scatter.19.cloned.1.call-start = ((), (), s32[]{:S(2)}) async-start(), calls=%async_computation.21 | async-start | bytes 9437184 | tf_op jit(solution)/shard_map/reduce_scatter | solution.py:45
  991.8 527.2 %reduce-scatter.21.cloned.1.call-start = ((), (), s32[]{:S(2)}) async-start(), calls=%async_computation.22 | async-start | bytes 9437184 | tf_op jit(solution)/shard_map/reduce_scatter | solution.py:45
  1062.7 287.2 %collective-permute-start.23 = (f32[768,2304]{1,0:T(8,128)}, f32[768,2304]{1,0:T(8,128)}, u32[]{:S(2)}, u32[]{:S(2)}) collective-permute-start(f32[768,2304]{1,0:T(8,128)} %token_sum_up.5), channel_id=1, source_target_pairs={{0,4},{4,0},{1,5},{5,1},{2,6},{6,2},{3,7},{7,3}} | collective-permute-start | bytes 21233672 | tf_op jit(solution)/shard_map/ppermute | solution.py:32
  1063.9 503.0 %reduce-scatter.23.cloned.1.call-start = ((), (), s32[]{:S(2)}) async-start(), calls=%async_computation.23 | async-start | bytes 9437184 | tf_op jit(solution)/shard_map/reduce_scatter | solution.py:45
  1217.0 307.6 %collective-permute-start.20 = (f32[768,4480]{1,0:T(8,128)}, f32[768,4480]{1,0:T(8,128)}, u32[]{:S(2)}, u32[]{:S(2)}) collective-permute-start(f32[768,4480]{1,0:T(8,128)} %token_sum_up.6), channel_id=1, source_target_pairs={{0,1},{1,0},{2,3},{3,2},{4,5},{5,4},{6,7},{7,6}} | collective-permute-start | bytes 41287688 | tf_op jit(solution)/shard_map/ppermute | solution.py:32
  1338.8 154.6 %collective-permute-start.24 = (f32[2304,768]{1,0:T(8,128)}, f32[2304,768]{1,0:T(8,128)}, u32[]{:S(2)}, u32[]{:S(2)}) collective-permute-start(f32[2304,768]{1,0:T(8,128)} %broadcast_select_fusion.10), channel_id=1, source_target_pairs={{0,4},{4,0},{1,5},{5,1},{2,6},{6,2},{3,7},{7,3}} | collective-permute-start | bytes 21233672 | tf_op jit(solution)/shard_map/ppermute | solution.py:32
  1346.4 147.9 %collective-permute-start.21 = (f32[2240,768]{1,0:T(8,128)}, f32[2240,768]{1,0:T(8,128)}, u32[]{:S(2)}, u32[]{:S(2)}) collective-permute-start(f32[2240,768]{1,0:T(8,128)} %constant_dynamic-slice_fusion), channel_id=1, source_target_pairs={{1,2},{2,1},{5,6},{6,5}} | collective-permute-start | bytes 20643848 | tf_op jit(solution)/shard_map/ppermute | solution.py:149
  (46 other events, 1936.1 us)
Sparse Core Ops, SparseCore 0:
  16.8 62.7 all-gather.8
  81.1 42.1 all-gather.10
  216.7 97.0 reduce-scatter.8
  315.9 80.4 reduce-scatter.10
  397.8 42.1 all-gather.16
  441.3 42.1 all-gather.12
  485.6 42.1 all-gather.14
  529.2 42.1 all-gather.18
  573.7 74.3 reduce-scatter.12
  650.2 74.3 reduce-scatter.14
  821.1 41.3 all-gather.20
  871.4 41.8 all-gather.22
  915.6 74.3 reduce-scatter.16
  992.1 74.3 reduce-scatter.18
  1068.6 108.5 reduce-scatter.20
  1350.0 107.3 reduce-scatter.22
